TPU v7x, 128 devices: a whole 4x4x4 slice. The times are simulated.
128 devices in a mesh: cp: 16 (over y, x), tp: 8 (over z, core).
Axes of the slice: x: 4, y: 4, z: 4, core: 2. Of those that a mesh axis runs over, the one named last changes fastest.
Arguments:
- tokens: bfloat16 [8192, 4096], P('cp'), may hold values from -150 to 150
- gain: bfloat16 [4096], replicated, may hold values from 0.099609375 to 1.8984375
- w_query: bfloat16 [4096, 4096], P(None, 'tp'), may hold values from -3 to 3
- w_key: bfloat16 [4096, 1024], P(None, 'tp'), may hold values from -1 to 1
- w_value: bfloat16 [4096, 1024], P(None, 'tp'), may hold values from -0.09375 to 0.09375
- w_out: bfloat16 [4096, 4096], P('tp'), may hold values from -0.09375 to 0.09375
- doc_ids: int32 [8192], replicated, may hold values from 0 to 15, as said below
Outputs:
- mixed: bfloat16 [8192, 4096], P('cp', 'tp')
Inputs may be any that keep to these rules, and one draw needn't show every extreme that they name: `doc_ids`: document numbers never fall along the sequence, and every number of the range is used; every document covers at most 2305 positions; two documents cover exactly 2305, each beginning at the first position of a stretch, one in the first 4096 positions and one starting in the last 4096.
All inputs are finite; a program needn't handle non-finite values.
Results may differ from a plain program's by a relative error of at most 0.015.
Values may be sent and summed in bfloat16 or wider, within the bound.
A program may use at most 128 MiB of HBM per device.

v0:
```python
import math

import jax
import jax.numpy as jnp
from jax import lax
from jax.sharding import PartitionSpec as P

HEADS = 32
KV_HEADS = 8
HD = 128


rope_theta = 500000.0
norm_epsilon = 1e-05
masked_score = -1e30


def passed_along(shard, axis, by):
    count = lax.axis_size(axis)
    pairs = [(i, i + by) for i in range(count) if 0 <= i + by < count]
    return lax.ppermute(shard, axis, pairs)


def in_blocks(shard, dim, count):
    shape = shard.shape
    pieces = shard.reshape(*shape[:dim], count, shape[dim] // count, *shape[dim + 1 :])
    return jnp.moveaxis(pieces, dim, 0)


def summed_on_arrival(shard, axis, dim):
    pieces = in_blocks(shard, dim, lax.axis_size(axis))
    arrived = lax.all_to_all(pieces, axis, split_axis=0, concat_axis=0, tiled=True)
    return arrived.astype(jnp.float32).sum(axis=0)


def global_positions(row_index, tok_dev, cp_size):
    half_rows = tok_dev // 2
    device = row_index // tok_dev
    within = row_index % tok_dev
    stretch_index = jnp.where(within < half_rows, device, 2 * cp_size - 1 - device)
    return stretch_index * half_rows + within % half_rows


def rotary(heads, positions):
    head_size = heads.shape[-1]
    half_size = head_size // 2
    index = jnp.arange(half_size).astype(jnp.float32)
    freqs = jnp.power(jnp.float32(rope_theta), -2.0 * index / head_size)
    angles = positions.astype(jnp.float32)[:, None] * freqs[None, :]
    cosine = jnp.cos(angles)[:, None, :]
    sine = jnp.sin(angles)[:, None, :]
    lower = heads[..., :half_size]
    upper = heads[..., half_size:]
    return jnp.concatenate([lower * cosine - upper * sine, upper * cosine + lower * sine], axis=-1)


def normalize(tokens, gain):
    widened = tokens.astype(jnp.float32)
    factor = lax.rsqrt(jnp.mean(widened * widened, axis=-1, keepdims=True) + norm_epsilon)
    return (widened * factor * gain.astype(jnp.float32)).astype(jnp.bfloat16)


def empty_state(query_count, kv_count, group_size):
    return (
        jnp.full((kv_count, group_size, query_count), masked_score, jnp.float32),
        jnp.zeros((kv_count, group_size, query_count), jnp.float32),
        jnp.zeros((query_count, kv_count, group_size, HD), jnp.float32),
    )


def finish(carry_state):
    running_max, weight_sum, accumulated = carry_state
    result = accumulated / jnp.transpose(weight_sum, (2, 0, 1))[..., None]
    return result.astype(jnp.bfloat16).reshape(result.shape[0], -1)


def attend(
    carry_state,
    queries,
    query_pos,
    query_doc,
    key_rows,
    value_rows,
    key_pos,
    key_doc,
    key_valid,
    scale,
):
    allowed = (
        (key_doc[None, :] == query_doc[:, None])
        & (key_pos[None, :] <= query_pos[:, None])
        & key_valid[None, :]
    )
    key_count = key_rows.shape[0]
    kv_count = queries.shape[1]
    head_size = queries.shape[3]

    def update(previous):
        running_max, weight_sum, accumulated = previous
        key_heads = key_rows.reshape(key_count, kv_count, head_size)
        value_heads = value_rows.reshape(key_count, kv_count, head_size)
        scores = (
            jnp.einsum("tkgd,skd->kgts", queries, key_heads, preferred_element_type=jnp.float32)
            * scale
        )
        scores = jnp.where(allowed[None, None], scores, masked_score)
        new_max = jnp.maximum(running_max, jnp.max(scores, axis=-1))
        weights = jnp.where(allowed[None, None], jnp.exp(scores - new_max[..., None]), 0.0)
        factor = jnp.exp(running_max - new_max)
        weight_sum = weight_sum * factor + jnp.sum(weights, axis=-1)
        added = jnp.einsum(
            "kgts,skd->tkgd",
            weights.astype(jnp.bfloat16),
            value_heads,
            preferred_element_type=jnp.float32,
        )
        accumulated = accumulated * jnp.transpose(factor, (2, 0, 1))[..., None] + added
        return (new_max, weight_sum, accumulated)

    def unchanged(previous):
        return previous

    return lax.cond(jnp.any(allowed), update, unchanged, carry_state)


def shards(tokens, gain, w_query, w_key, w_value, w_out, doc_ids):
    cp_size = lax.axis_size("cp")
    tok_dev = tokens.shape[0]
    half_rows = tok_dev // 2
    device = lax.axis_index("cp")
    group_size = HEADS // KV_HEADS
    scale = 1.0 / math.sqrt(HD)
    reach_count = cp_size // 2 + 1
    normed = normalize(tokens, gain)
    query_pos = global_positions(
        device * tok_dev + jnp.arange(tok_dev, dtype=jnp.int32), tok_dev, cp_size
    )
    query_doc = jnp.take(doc_ids, query_pos)
    query = jnp.dot(normed, w_query, preferred_element_type=jnp.float32)
    head_count = query.shape[1] // HD
    kv_count = head_count // group_size
    query = rotary(query.reshape(tok_dev, head_count, HD), query_pos).astype(jnp.bfloat16)
    query = query.reshape(tok_dev, kv_count, group_size, HD)
    keys = jnp.dot(normed, w_key, preferred_element_type=jnp.float32)
    keys = (
        rotary(keys.reshape(tok_dev, kv_count, HD), query_pos)
        .astype(jnp.bfloat16)
        .reshape(tok_dev, kv_count * HD)
    )
    values = jnp.dot(normed, w_value, preferred_element_type=jnp.float32).astype(jnp.bfloat16)
    stacked = jnp.stack([keys, values])
    lower = stacked[:, :half_rows]
    upper = stacked[:, half_rows:]
    is_last = device == cp_size - 1
    offsets = jnp.arange(half_rows, dtype=jnp.int32)
    all_valid = jnp.ones((half_rows,), jnp.bool_)
    lower_query, upper_query = (query[:half_rows], query[half_rows:])
    lower_qpos, upper_qpos = (query_pos[:half_rows], query_pos[half_rows:])
    lower_qdoc, upper_qdoc = (query_doc[:half_rows], query_doc[half_rows:])
    lower_state = attend(
        empty_state(half_rows, kv_count, group_size),
        lower_query,
        lower_qpos,
        lower_qdoc,
        lower[0],
        lower[1],
        lower_qpos,
        lower_qdoc,
        all_valid,
        scale,
    )
    upper_state = attend(
        empty_state(half_rows, kv_count, group_size),
        upper_query,
        upper_qpos,
        upper_qdoc,
        upper[0],
        upper[1],
        upper_qpos,
        upper_qdoc,
        all_valid,
        scale,
    )
    for distance in range(1, reach_count + 1):
        moved_lower = passed_along(lower, "cp", 1)
        moved_upper = passed_along(upper, "cp", -1)
        upper = jnp.where(is_last, lower, moved_upper)
        lower = moved_lower
        lower_kpos = (device - distance) * half_rows + offsets
        upper_kpos = (2 * cp_size - 1 - device - distance) * half_rows + offsets
        lower_state = attend(
            lower_state,
            lower_query,
            lower_qpos,
            lower_qdoc,
            lower[0],
            lower[1],
            lower_kpos,
            jnp.take(doc_ids, jnp.maximum(lower_kpos, 0)),
            lower_kpos >= 0,
            scale,
        )
        upper_state = attend(
            upper_state,
            upper_query,
            upper_qpos,
            upper_qdoc,
            upper[0],
            upper[1],
            upper_kpos,
            jnp.take(doc_ids, jnp.maximum(upper_kpos, 0)),
            upper_kpos >= 0,
            scale,
        )
    attention = jnp.concatenate([finish(lower_state), finish(upper_state)], axis=0)
    partial_value = jnp.dot(attention, w_out, preferred_element_type=jnp.float32)
    mixed = summed_on_arrival(partial_value.astype(jnp.bfloat16), "tp", 1)
    return mixed.astype(jnp.bfloat16)


def solution(mesh):
    in_specs = (P("cp", None), P(), P(None, "tp"), P(None, "tp"), P(None, "tp"), P("tp", None), P())
    out_specs = P("cp", "tp")
    return jax.shard_map(shards, mesh=mesh, in_specs=in_specs, out_specs=out_specs, check_vma=False)
```

profile of v0, /device:TPU:16, one launch (start us, length us, event | category | flops | bytes accessed | tf_op | source)
XLA Modules:
  0.0 285.9 jit_solution(8804924408364114756)
XLA Ops:
  0.1 3.2 %fusion.296 = f32[512]{0:T(512)S(1)} fusion(bf16[512,4096]{1,0:T(8,128)(2,1)} %param.49), kind=kLoop, calls=%fused_computation.426 | loop fusion | flops 6290944 | bytes 4196352 | tf_op jit(solution)/shard_map/reduce_sum | solution.py:59
  8.4 4.5 %collective-permute-start.9 = (bf16[2,256,128]{1,2,0:T(8,128)(2,1)}, bf16[2,256,128]{1,2,0:T(8,128)(2,1)}, u32[]{:S(2)}, u32[]{:S(2)}) collective-permute-start(bf16[2,256,128]{1,2,0:T(8,128)(2,1)} %slice.295), channel_id=1, source_target_pairs={{8,0},{16,8},{24,16},{32,24},{40,32},{48,40},{56,48},{64,56},{72,6... | collective-permute-start | bytes 393224 | tf_op jit(solution)/shard_map/ppermute | solution.py:21
  19.5 1.9 multiply_cosine_fusion
  21.4 3.1 %gather_fusion = s32[512]{0:T(512)S(1)} fusion(s32[8192]{0:T(1024)S(1)} %copy-done.2, s32[1024]{0:T(1024)S(1)} %pad_clamp_fusion.17), kind=kCustom, calls=%fused_computation.18 | custom fusion | bytes 6144 | tf_op jit(solution)/shard_map/jit(_take)/gather | solution.py:138
  24.6 1.7 gather_fusion.18
  26.4 1.7 gather_fusion.17
  30.5 1.7 gather_fusion.15
  32.2 1.7 gather_fusion.14
  34.0 1.7 gather_fusion.13
  35.8 1.7 gather_fusion.12
  37.5 1.7 gather_fusion.11
  43.9 1.7 gather_fusion.8
  45.7 1.7 gather_fusion.7
  47.4 1.7 gather_fusion.6
  49.2 1.7 gather_fusion.5
  52.7 1.7 gather_fusion.3
  59.1 5.9 %fusion.365 = f32[512,512]{0,1:T(8,128)S(1)} fusion(bf16[4096,512]{1,0:T(8,128)(2,1)} %param.51, bf16[512,4096]{1,0:T(8,128)(2,1)} %param.49, f32[4096]{0:T(1024)S(1)} %convert_element_type.183, f32[512]{0:T(512)S(1)} %add_rsqrt_fusion), kind=kOutput, calls=%fused_computation.622 | convolution fusion | flops 2155872256 | bytes 9455616 | tf_op jit(solution)/shard_map/dot_general | solution.py:139
  67.1 2.6 fusion.370
  69.7 3.4 %compare_and_fusion.1 = (pred[256,256]{0,1:T(8,128)(4,1)}, pred[]{:T(512)}, pred[]{:T(512)}, pred[256,256]{0,1:T(8,128)(4,1)S(1)}, pred[]{:T(512)}, /*index=5*/p...) fusion(s32[256]{0:T(256)S(1)} %get-tuple-element.1221, ...), kind=kLoop, calls=%fused_computation.460 | loop fusion | flops 1900538 | bytes 406790 | tf_op jit(solution)/shard_map/and | solution.py:90
  73.1 2.2 compare_and_fusion
  75.4 3.0 %fusion.379 = (pred[]{:T(512)}, pred[256,256]{0,1:T(8,128)(4,1)}, pred[]{:T(512)}, pred[256,256]{0,1:T(8,128)(4,1)}, pred[]{:T(512)}, /*index=5*/pred[256,256]{0...) fusion(pred[256]{0:T(512)(128)(4,1)} %get-tuple-element.1254, s32[256]{0:T(256)S(1)} %get-tuple-element.1222, ...), kind=kLoop, calls=%fused_computation.632 | loop fusion | flops 1310716 | bytes 273412 | tf_op jit(solution)/shard_map/reduce_or | solution.py:123
  91.2 4.0 %conditional.30 = (f32[1,4,256]{2,1,0:T(4,128)}, f32[1,4,256]{2,1,0:T(4,128)S(1)}, f32[256,1,4,128]{3,0,2,1:T(8,128)S(1)}) conditional(s32[]{:T(128)} %convert_element_type.198, () %tuple.144, (pred[256,256]{0,1:T(8,128)(4,1)S(1)}, bf16[1,256,128]{1,2,0:T(8,128)(2,1)}, bf16[256,1,4,128]{3,0,2,1:T(8,128)(2,1)S(1)}, ...), branch_computations={%region_61.63_spmd, %region_62.66_spmd} | conditional | flops 136713216 | bytes 4313112 | solution.py:123
  95.2 4.0 %conditional.20 = (f32[1,4,256]{2,1,0:T(4,128)}, f32[1,4,256]{2,1,0:T(4,128)S(1)}, f32[256,1,4,128]{3,0,2,1:T(8,128)S(1)}) conditional(s32[]{:T(128)} %convert_element_type.181, () %tuple.132, (pred[256,256]{0,1:T(8,128)(4,1)S(1)}, bf16[1,256,128]{1,2,0:T(8,128)(2,1)}, bf16[256,1,4,128]{3,0,2,1:T(8,128)(2,1)S(1)}, ...), branch_computations={%region_11.13_spmd, %region_12.16_spmd} | conditional | flops 136713216 | bytes 4313112 | solution.py:123
  100.2 1.9 collective-permute-start
  102.1 6.0 %collective-permute-start.10 = (bf16[2,256,128]{1,2,0:T(8,128)(2,1)S(1)}, bf16[2,256,128]{1,2,0:T(8,128)(2,1)S(1)}, u32[]{:S(2)}, u32[]{:S(2)}) collective-permute-start(bf16[2,256,128]{1,2,0:T(8,128)(2,1)S(1)} %get-tuple-element.1166), channel_id=1, source_target_pairs={{8,0},{16,8},{24,16},{32,24},{40,32},{48,40},{56,48},{64,56},{72,6... | collective-permute-start | bytes 393224 | tf_op jit(solution)/shard_map/ppermute | solution.py:21
  108.2 3.1 %conditional.31 = ((f32[1,4,256]{2,1,0:T(4,128)}, f32[1,4,256]{2,1,0:T(4,128)S(1)}, f32[256,1,4,128]{3,0,2,1:T(8,128)S(1)})) conditional(s32[]{:T(128)} %convert_element_type.197, (f32[1,4,256]{2,1,0:T(4,128)}, f32[1,4,256]{2,1,0:T(4,128)S(1)}, f32[256,1,4,128]{3,0,2,1:T(8,128)S(1)}) %conditional.30, (pred[256,256]{0,1:T(8,128)(4,1)S(1)}, ...), branch_computations={%region_65.67_spmd, %region_66.70_spmd} | conditional | flops 136842240 | bytes 4849696 | solution.py:123
  111.3 5.9 %collective-permute-start.11 = (bf16[2,256,128]{1,2,0:T(8,128)(2,1)S(1)}, bf16[2,256,128]{1,2,0:T(8,128)(2,1)S(1)}, u32[]{:S(2)}, u32[]{:S(2)}) collective-permute-start(bf16[2,256,128]{1,2,0:T(8,128)(2,1)S(1)} %broadcast_select_fusion.7), channel_id=1, source_target_pairs={{8,0},{16,8},{24,16},{32,24},{40,32},{48,40},{56,48},{64,56},{72,6... | collective-permute-start | bytes 393224 | tf_op jit(solution)/shard_map/ppermute | solution.py:21
  117.2 3.1 %conditional.32 = ((f32[1,4,256]{2,1,0:T(4,128)}, f32[1,4,256]{2,1,0:T(4,128)S(1)}, f32[256,1,4,128]{3,0,2,1:T(8,128)S(1)})) conditional(s32[]{:T(128)} %convert_element_type.196, (f32[1,4,256]{2,1,0:T(4,128)}, f32[1,4,256]{2,1,0:T(4,128)S(1)}, f32[256,1,4,128]{3,0,2,1:T(8,128)S(1)}) %get-tuple-element.1421, (pred[256,256]{0,1:T(8,128)(4,1)S(1)}, ...), branch_computations={%region_69.71_spmd, %region_70.74_spmd} | conditional | flops 136842240 | bytes 4849696 | solution.py:123
  120.2 1.9 collective-permute-start.1
  122.2 3.1 %conditional.21 = ((f32[1,4,256]{2,1,0:T(4,128)}, f32[1,4,256]{2,1,0:T(4,128)S(1)}, f32[256,1,4,128]{3,0,2,1:T(8,128)S(1)})) conditional(s32[]{:T(128)} %convert_element_type.180, (f32[1,4,256]{2,1,0:T(4,128)}, f32[1,4,256]{2,1,0:T(4,128)S(1)}, f32[256,1,4,128]{3,0,2,1:T(8,128)S(1)}) %conditional.20, (pred[256,256]{0,1:T(8,128)(4,1)S(1)}, ...), branch_computations={%region_15.17_spmd, %region_16.20_spmd} | conditional | flops 136842240 | bytes 4849696 | solution.py:123
  125.2 3.9 %collective-permute-done.1 = bf16[2,256,128]{1,2,0:T(8,128)(2,1)S(1)} collective-permute-done((bf16[2,256,128]{1,2,0:T(8,128)(2,1)S(1)}, bf16[2,256,128]{1,2,0:T(8,128)(2,1)S(1)}, u32[]{:S(2)}, u32[]{:S(2)}) %collective-permute-start.1) | collective-permute-done | bytes 131104 | tf_op jit(solution)/shard_map/ppermute | solution.py:21
  129.2 2.1 collective-permute-start.12
  131.3 3.1 %conditional.33 = ((f32[1,4,256]{2,1,0:T(4,128)}, f32[1,4,256]{2,1,0:T(4,128)S(1)}, f32[256,1,4,128]{3,0,2,1:T(8,128)S(1)})) conditional(s32[]{:T(128)} %convert_element_type.195, (f32[1,4,256]{2,1,0:T(4,128)}, f32[1,4,256]{2,1,0:T(4,128)S(1)}, f32[256,1,4,128]{3,0,2,1:T(8,128)S(1)}) %get-tuple-element.1422, (pred[256,256]{0,1:T(8,128)(4,1)S(1)}, ...), branch_computations={%region_73.75_spmd, %region_74.78_spmd} | conditional | flops 136842240 | bytes 4849696 | solution.py:123
  134.4 3.7 %collective-permute-start.2 = (bf16[2,256,128]{1,2,0:T(8,128)(2,1)S(1)}, bf16[2,256,128]{1,2,0:T(8,128)(2,1)S(1)}, u32[]{:S(2)}, u32[]{:S(2)}) collective-permute-start(bf16[2,256,128]{1,2,0:T(8,128)(2,1)S(1)} %collective-permute-done.1), channel_id=1, source_target_pairs={{0,8},{8,16},{16,24},{24,32},{32,40},{40,48},{48,56},{56,64},{64,7... | collective-permute-start | bytes 393224 | tf_op jit(solution)/shard_map/ppermute | solution.py:21
  138.2 3.1 %conditional.22 = ((f32[1,4,256]{2,1,0:T(4,128)}, f32[1,4,256]{2,1,0:T(4,128)S(1)}, f32[256,1,4,128]{3,0,2,1:T(8,128)S(1)})) conditional(s32[]{:T(128)} %convert_element_type.179, (f32[1,4,256]{2,1,0:T(4,128)}, f32[1,4,256]{2,1,0:T(4,128)S(1)}, f32[256,1,4,128]{3,0,2,1:T(8,128)S(1)}) %get-tuple-element.1413, (pred[256,256]{0,1:T(8,128)(4,1)S(1)}, ...), branch_computations={%region_19.21_spmd, %region_20.24_spmd} | conditional | flops 136842240 | bytes 4849696 | solution.py:123
  141.2 2.1 collective-permute-done.2
  143.4 2.1 collective-permute-start.13
  145.5 3.1 %conditional.34 = ((f32[1,4,256]{2,1,0:T(4,128)}, f32[1,4,256]{2,1,0:T(4,128)S(1)}, f32[256,1,4,128]{3,0,2,1:T(8,128)S(1)})) conditional(s32[]{:T(128)} %convert_element_type.194, (f32[1,4,256]{2,1,0:T(4,128)}, f32[1,4,256]{2,1,0:T(4,128)S(1)}, f32[256,1,4,128]{3,0,2,1:T(8,128)S(1)}) %get-tuple-element.1423, (pred[256,256]{0,1:T(8,128)(4,1)S(1)}, ...), branch_computations={%region_77.79_spmd, %region_78.82_spmd} | conditional | flops 136842240 | bytes 4849696 | solution.py:123
  148.6 3.7 %collective-permute-start.3 = (bf16[2,256,128]{1,2,0:T(8,128)(2,1)S(1)}, bf16[2,256,128]{1,2,0:T(8,128)(2,1)S(1)}, u32[]{:S(2)}, u32[]{:S(2)}) collective-permute-start(bf16[2,256,128]{1,2,0:T(8,128)(2,1)S(1)} %collective-permute-done.2), channel_id=1, source_target_pairs={{0,8},{8,16},{16,24},{24,32},{32,40},{40,48},{48,56},{56,64},{64,7... | collective-permute-start | bytes 393224 | tf_op jit(solution)/shard_map/ppermute | solution.py:21
  152.3 3.1 %conditional.23 = ((f32[1,4,256]{2,1,0:T(4,128)}, f32[1,4,256]{2,1,0:T(4,128)S(1)}, f32[256,1,4,128]{3,0,2,1:T(8,128)S(1)})) conditional(s32[]{:T(128)} %convert_element_type.178, (f32[1,4,256]{2,1,0:T(4,128)}, f32[1,4,256]{2,1,0:T(4,128)S(1)}, f32[256,1,4,128]{3,0,2,1:T(8,128)S(1)}) %get-tuple-element.1414, (pred[256,256]{0,1:T(8,128)(4,1)S(1)}, ...), branch_computations={%region_23.25_spmd, %region_24.28_spmd} | conditional | flops 136842240 | bytes 4849696 | solution.py:123
  155.4 2.1 collective-permute-done.3
  157.6 2.1 collective-permute-start.14
  159.6 3.1 %conditional.35 = ((f32[1,4,256]{2,1,0:T(4,128)}, f32[1,4,256]{2,1,0:T(4,128)S(1)}, f32[256,1,4,128]{3,0,2,1:T(8,128)S(1)})) conditional(s32[]{:T(128)} %convert_element_type.193, (f32[1,4,256]{2,1,0:T(4,128)}, f32[1,4,256]{2,1,0:T(4,128)S(1)}, f32[256,1,4,128]{3,0,2,1:T(8,128)S(1)}) %get-tuple-element.1424, (pred[256,256]{0,1:T(8,128)(4,1)S(1)}, ...), branch_computations={%region_81.83_spmd, %region_82.86_spmd} | conditional | flops 136842240 | bytes 4849696 | solution.py:123
  162.7 3.8 %collective-permute-start.4 = (bf16[2,256,128]{1,2,0:T(8,128)(2,1)S(1)}, bf16[2,256,128]{1,2,0:T(8,128)(2,1)S(1)}, u32[]{:S(2)}, u32[]{:S(2)}) collective-permute-start(bf16[2,256,128]{1,2,0:T(8,128)(2,1)S(1)} %collective-permute-done.3), channel_id=1, source_target_pairs={{0,8},{8,16},{16,24},{24,32},{32,40},{40,48},{48,56},{56,64},{64,7... | collective-permute-start | bytes 393224 | tf_op jit(solution)/shard_map/ppermute | solution.py:21
  166.5 3.4 %conditional.24 = ((f32[1,4,256]{2,1,0:T(4,128)}, f32[1,4,256]{2,1,0:T(4,128)S(1)}, f32[256,1,4,128]{3,0,2,1:T(8,128)S(1)})) conditional(s32[]{:T(128)} %convert_element_type.177, (f32[1,4,256]{2,1,0:T(4,128)}, f32[1,4,256]{2,1,0:T(4,128)S(1)}, f32[256,1,4,128]{3,0,2,1:T(8,128)S(1)}) %get-tuple-element.1415, (pred[256,256]{0,1:T(8,128)(4,1)S(1)}, ...), branch_computations={%region_27.29_spmd, %region_28.32_spmd} | conditional | flops 136842240 | bytes 4849696 | solution.py:123
  169.9 1.7 collective-permute-done.4
  171.7 2.5 collective-permute-start.15
  174.2 3.1 %conditional.36 = ((f32[1,4,256]{2,1,0:T(4,128)}, f32[1,4,256]{2,1,0:T(4,128)S(1)}, f32[256,1,4,128]{3,0,2,1:T(8,128)S(1)})) conditional(s32[]{:T(128)} %convert_element_type.192, (f32[1,4,256]{2,1,0:T(4,128)}, f32[1,4,256]{2,1,0:T(4,128)S(1)}, f32[256,1,4,128]{3,0,2,1:T(8,128)S(1)}) %get-tuple-element.1425, (pred[256,256]{0,1:T(8,128)(4,1)S(1)}, ...), branch_computations={%region_85.87_spmd, %region_86.90_spmd} | conditional | flops 136842240 | bytes 4849696 | solution.py:123
  177.3 3.3 %collective-permute-start.5 = (bf16[2,256,128]{1,2,0:T(8,128)(2,1)S(1)}, bf16[2,256,128]{1,2,0:T(8,128)(2,1)S(1)}, u32[]{:S(2)}, u32[]{:S(2)}) collective-permute-start(bf16[2,256,128]{1,2,0:T(8,128)(2,1)S(1)} %collective-permute-done.4), channel_id=1, source_target_pairs={{0,8},{8,16},{16,24},{24,32},{32,40},{40,48},{48,56},{56,64},{64,7... | collective-permute-start | bytes 393224 | tf_op jit(solution)/shard_map/ppermute | solution.py:21
  180.6 3.1 %conditional.25 = ((f32[1,4,256]{2,1,0:T(4,128)}, f32[1,4,256]{2,1,0:T(4,128)S(1)}, f32[256,1,4,128]{3,0,2,1:T(8,128)S(1)})) conditional(s32[]{:T(128)} %convert_element_type.176, (f32[1,4,256]{2,1,0:T(4,128)}, f32[1,4,256]{2,1,0:T(4,128)S(1)}, f32[256,1,4,128]{3,0,2,1:T(8,128)S(1)}) %get-tuple-element.1416, (pred[256,256]{0,1:T(8,128)(4,1)S(1)}, ...), branch_computations={%region_31.33_spmd, %region_32.36_spmd} | conditional | flops 136842240 | bytes 4849696 | solution.py:123
  183.7 2.5 collective-permute-done.5
  186.3 2.1 collective-permute-start.16
  188.4 3.1 %conditional.37 = ((f32[1,4,256]{2,1,0:T(4,128)}, f32[1,4,256]{2,1,0:T(4,128)S(1)}, f32[256,1,4,128]{3,0,2,1:T(8,128)S(1)})) conditional(s32[]{:T(128)} %convert_element_type.191, (f32[1,4,256]{2,1,0:T(4,128)}, f32[1,4,256]{2,1,0:T(4,128)S(1)}, f32[256,1,4,128]{3,0,2,1:T(8,128)S(1)}) %get-tuple-element.1426, (pred[256,256]{0,1:T(8,128)(4,1)S(1)}, ...), branch_computations={%region_89.91_spmd, %region_90.94_spmd} | conditional | flops 136842240 | bytes 4849696 | solution.py:123
  191.4 1.9 collective-permute-start.6
  193.3 3.1 %conditional.26 = ((f32[1,4,256]{2,1,0:T(4,128)}, f32[1,4,256]{2,1,0:T(4,128)S(1)}, f32[256,1,4,128]{3,0,2,1:T(8,128)S(1)})) conditional(s32[]{:T(128)} %convert_element_type.175, (f32[1,4,256]{2,1,0:T(4,128)}, f32[1,4,256]{2,1,0:T(4,128)S(1)}, f32[256,1,4,128]{3,0,2,1:T(8,128)S(1)}) %get-tuple-element.1417, (pred[256,256]{0,1:T(8,128)(4,1)S(1)}, ...), branch_computations={%region_35.37_spmd, %region_36.40_spmd} | conditional | flops 136842240 | bytes 4849696 | solution.py:123
  196.4 4.0 %collective-permute-done.6 = bf16[2,256,128]{1,2,0:T(8,128)(2,1)S(1)} collective-permute-done((bf16[2,256,128]{1,2,0:T(8,128)(2,1)S(1)}, bf16[2,256,128]{1,2,0:T(8,128)(2,1)S(1)}, u32[]{:S(2)}, u32[]{:S(2)}) %collective-permute-start.6) | collective-permute-done | bytes 131104 | tf_op jit(solution)/shard_map/ppermute | solution.py:21
  201.0 1.9 collective-permute-start.17
  203.0 3.9 %collective-permute-start.7 = (bf16[2,256,128]{1,2,0:T(8,128)(2,1)S(1)}, bf16[2,256,128]{1,2,0:T(8,128)(2,1)S(1)}, u32[]{:S(2)}, u32[]{:S(2)}) collective-permute-start(bf16[2,256,128]{1,2,0:T(8,128)(2,1)S(1)} %collective-permute-done.6), channel_id=1, source_target_pairs={{0,8},{8,16},{16,24},{24,32},{32,40},{40,48},{48,56},{56,64},{64,7... | collective-permute-start | bytes 393224 | tf_op jit(solution)/shard_map/ppermute | solution.py:21
  207.0 5.3 %collective-permute-done.7 = bf16[2,256,128]{1,2,0:T(8,128)(2,1)S(1)} collective-permute-done((bf16[2,256,128]{1,2,0:T(8,128)(2,1)S(1)}, bf16[2,256,128]{1,2,0:T(8,128)(2,1)S(1)}, u32[]{:S(2)}, u32[]{:S(2)}) %collective-permute-start.7) | collective-permute-done | bytes 131104 | tf_op jit(solution)/shard_map/ppermute | solution.py:21
  212.5 2.2 collective-permute-start.8
  214.8 6.7 %collective-permute-done.8 = bf16[2,256,128]{1,2,0:T(8,128)(2,1)S(1)} collective-permute-done((bf16[2,256,128]{1,2,0:T(8,128)(2,1)S(1)}, bf16[2,256,128]{1,2,0:T(8,128)(2,1)S(1)}, u32[]{:S(2)}, u32[]{:S(2)}) %collective-permute-start.8) | collective-permute-done | bytes 131104 | tf_op jit(solution)/shard_map/ppermute | solution.py:21
  221.9 4.6 %convolution_convert_fusion = bf16[512,4096]{1,0:T(8,128)(2,1)S(1)} fusion(bf16[512,4096]{1,0:T(8,128)(2,1)} %param.54, bf16[256,512]{0,1:T(8,128)(2,1)S(1)} %bitcast.920, bf16[256,512]{0,1:T(8,128)(2,1)S(1)} %bitcast.921), kind=kOutput, calls=%fused_computation.429 | convolution fusion | flops 2150629376 | bytes 8912896 | tf_op jit(solution)/shard_map/dot_general | solution.py:216
  226.9 55.0 %all_to_all.5 = bf16[8,512,512]{2,1,0:T(8,128)(2,1)} all-to-all(bf16[8,512,512]{2,1,0:T(8,128)(2,1)S(1)} %bitcast.919), channel_id=1, replica_groups=mesh['cp'=16,'tp'=8] {'tp'}, dimensions={0} | all-to-all | bytes 8388608 | tf_op jit(solution)/shard_map/all_to_all | solution.py:32
  281.9 3.7 %reduce_sum.242 = bf16[512,512]{1,0:T(8,128)(2,1)} reduce(bf16[8,512,512]{2,1,0:T(8,128)(2,1)} %all_to_all.5, bf16[]{:T(256)} %constant.327.clone.1), dimensions={0}, to_apply=%region_101.103 | reduce | flops 1835008 | bytes 4718594 | tf_op jit(solution)/shard_map/reduce_sum | solution.py:33
  (256 shorter events, 78.1 us)
Async XLA Ops:
  0.0 3.3 %copy-start = (bf16[4096,128]{1,0:T(8,128)(2,1)S(1)}, bf16[4096,128]{1,0:T(8,128)(2,1)}, u32[]{:S(2)}) copy-start(bf16[4096,128]{1,0:T(8,128)(2,1)} %param.53) | copy-start | bytes 3145732
  0.0 3.3 %copy-start.11 = (bf16[4096]{0:T(1024)(128)(2,1)S(1)}, bf16[4096]{0:T(1024)(128)(2,1)}, u32[]{:S(2)}) copy-start(bf16[4096]{0:T(1024)(128)(2,1)} %param.50) | copy-start | bytes 24580
  0.0 3.8 %copy-start.3 = (bf16[512,4096]{1,0:T(8,128)(2,1)S(1)}, bf16[512,4096]{1,0:T(8,128)(2,1)}, u32[]{:S(2)}) copy-start(bf16[512,4096]{1,0:T(8,128)(2,1)} %param.49) | copy-start | bytes 12582916
  3.8 1.6 copy-start.16
  5.4 16.0 %copy-start.2 = (s32[8192]{0:T(1024)S(1)}, s32[8192]{0:T(1024)}, u32[]{:S(2)}) copy-start(s32[8192]{0:T(1024)} %param.55) | copy-start | bytes 98308
  7.7 26.3 %copy-start.8 = (bf16[2,512,128]{1,2,0:T(8,128)(2,1)}, bf16[2,512,128]{1,2,0:T(8,128)(2,1)S(1)}, u32[]{:S(2)}) copy-start(bf16[2,512,128]{1,2,0:T(8,128)(2,1)S(1)} %pad_maximum_fusion.1) | copy-start | bytes 786436
  8.4 90.8 %collective-permute-start.9 = (bf16[2,256,128]{1,2,0:T(8,128)(2,1)}, bf16[2,256,128]{1,2,0:T(8,128)(2,1)}, u32[]{:S(2)}, u32[]{:S(2)}) collective-permute-start(bf16[2,256,128]{1,2,0:T(8,128)(2,1)} %slice.295), channel_id=1, source_target_pairs={{8,0},{16,8},{24,16},{32,24},{40,32},{48,40},{56,48},{64,56},{72,6... | collective-permute-start | bytes 393224 | tf_op jit(solution)/shard_map/ppermute | solution.py:21
  65.0 2.1 copy-start.12
  65.0 2.1 copy-start.13
  65.0 4.7 %copy-start.14 = (pred[256]{0:T(512)(128)(4,1)S(1)}, pred[256]{0:T(512)(128)(4,1)}, u32[]{:S(2)}) copy-start(pred[256]{0:T(512)(128)(4,1)} %get-tuple-element.1293) | copy-start | bytes 772
  65.0 4.7 %copy-start.15 = (pred[256]{0:T(512)(128)(4,1)S(1)}, pred[256]{0:T(512)(128)(4,1)}, u32[]{:S(2)}) copy-start(pred[256]{0:T(512)(128)(4,1)} %get-tuple-element.1294) | copy-start | bytes 772
  91.2 4.1 %copy-start.10 = (pred[256,256]{0,1:T(8,128)(4,1)S(1)}, pred[256,256]{0,1:T(8,128)(4,1)}, u32[]{:S(2)}) copy-start(pred[256,256]{0,1:T(8,128)(4,1)} %get-tuple-element.1201) | copy-start | bytes 196612
  91.2 8.0 %copy-start.9 = (bf16[2,512,128]{1,2,0:T(8,128)(2,1)S(1)}, bf16[2,512,128]{1,2,0:T(8,128)(2,1)}, u32[]{:S(2)}) copy-start(bf16[2,512,128]{1,2,0:T(8,128)(2,1)} %copy-done.8) | copy-start | bytes 786436
  91.2 17.0 %copy-start.7 = (pred[256,256]{0,1:T(8,128)(4,1)S(1)}, pred[256,256]{0,1:T(8,128)(4,1)}, u32[]{:S(2)}) copy-start(pred[256,256]{0,1:T(8,128)(4,1)} %get-tuple-element.1096) | copy-start | bytes 196612
  99.2 17.9 %copy-start.6 = (pred[256,256]{0,1:T(8,128)(4,1)S(1)}, pred[256,256]{0,1:T(8,128)(4,1)}, u32[]{:S(2)}) copy-start(pred[256,256]{0,1:T(8,128)(4,1)} %get-tuple-element.1236) | copy-start | bytes 196612
  100.2 11.1 %collective-permute-start = (bf16[2,256,128]{1,2,0:T(8,128)(2,1)S(1)}, bf16[2,256,128]{1,2,0:T(8,128)(2,1)S(1)}, u32[]{:S(2)}, u32[]{:S(2)}) collective-permute-start(bf16[2,256,128]{1,2,0:T(8,128)(2,1)S(1)} %get-tuple-element.1165), channel_id=1, source_target_pairs={{0,8},{8,16},{16,24},{24,32},{32,40},{40,48},{48,56},{56,64},{64,7... | collective-permute-start | bytes 393224 | tf_op jit(solution)/shard_map/ppermute | solution.py:21
  102.1 9.1 %collective-permute-start.10 = (bf16[2,256,128]{1,2,0:T(8,128)(2,1)S(1)}, bf16[2,256,128]{1,2,0:T(8,128)(2,1)S(1)}, u32[]{:S(2)}, u32[]{:S(2)}) collective-permute-start(bf16[2,256,128]{1,2,0:T(8,128)(2,1)S(1)} %get-tuple-element.1166), channel_id=1, source_target_pairs={{8,0},{16,8},{24,16},{32,24},{40,32},{48,40},{56,48},{64,56},{72,6... | collective-permute-start | bytes 393224 | tf_op jit(solution)/shard_map/ppermute | solution.py:21
  108.2 14.0 %copy-start.5 = (pred[256,256]{0,1:T(8,128)(4,1)S(1)}, pred[256,256]{0,1:T(8,128)(4,1)}, u32[]{:S(2)}) copy-start(pred[256,256]{0,1:T(8,128)(4,1)} %get-tuple-element.1078) | copy-start | bytes 196612
  111.3 17.9 %collective-permute-start.11 = (bf16[2,256,128]{1,2,0:T(8,128)(2,1)S(1)}, bf16[2,256,128]{1,2,0:T(8,128)(2,1)S(1)}, u32[]{:S(2)}, u32[]{:S(2)}) collective-permute-start(bf16[2,256,128]{1,2,0:T(8,128)(2,1)S(1)} %broadcast_select_fusion.7), channel_id=1, source_target_pairs={{8,0},{16,8},{24,16},{32,24},{40,32},{48,40},{56,48},{64,56},{72,6... | collective-permute-start | bytes 393224 | tf_op jit(solution)/shard_map/ppermute | solution.py:21
  120.2 9.0 %collective-permute-start.1 = (bf16[2,256,128]{1,2,0:T(8,128)(2,1)S(1)}, bf16[2,256,128]{1,2,0:T(8,128)(2,1)S(1)}, u32[]{:S(2)}, u32[]{:S(2)}) collective-permute-start(bf16[2,256,128]{1,2,0:T(8,128)(2,1)S(1)} %collective-permute-done), channel_id=1, source_target_pairs={{0,8},{8,16},{16,24},{24,32},{32,40},{40,48},{48,56},{56,64},{64,7... | collective-permute-start | bytes 393224 | tf_op jit(solution)/shard_map/ppermute | solution.py:21
  122.2 16.0 %copy-start.4 = (pred[256,256]{0,1:T(8,128)(4,1)S(1)}, pred[256,256]{0,1:T(8,128)(4,1)}, u32[]{:S(2)}) copy-start(pred[256,256]{0,1:T(8,128)(4,1)} %get-tuple-element.1214) | copy-start | bytes 196612
  129.2 14.1 %collective-permute-start.12 = (bf16[2,256,128]{1,2,0:T(8,128)(2,1)S(1)}, bf16[2,256,128]{1,2,0:T(8,128)(2,1)S(1)}, u32[]{:S(2)}, u32[]{:S(2)}) collective-permute-start(bf16[2,256,128]{1,2,0:T(8,128)(2,1)S(1)} %broadcast_select_fusion.6), channel_id=1, source_target_pairs={{8,0},{16,8},{24,16},{32,24},{40,32},{48,40},{56,48},{64,56},{72,6... | collective-permute-start | bytes 393224 | tf_op jit(solution)/shard_map/ppermute | solution.py:21
  134.4 9.0 %collective-permute-start.2 = (bf16[2,256,128]{1,2,0:T(8,128)(2,1)S(1)}, bf16[2,256,128]{1,2,0:T(8,128)(2,1)S(1)}, u32[]{:S(2)}, u32[]{:S(2)}) collective-permute-start(bf16[2,256,128]{1,2,0:T(8,128)(2,1)S(1)} %collective-permute-done.1), channel_id=1, source_target_pairs={{0,8},{8,16},{16,24},{24,32},{32,40},{40,48},{48,56},{56,64},{64,7... | collective-permute-start | bytes 393224 | tf_op jit(solution)/shard_map/ppermute | solution.py:21
  143.4 14.1 %collective-permute-start.13 = (bf16[2,256,128]{1,2,0:T(8,128)(2,1)S(1)}, bf16[2,256,128]{1,2,0:T(8,128)(2,1)S(1)}, u32[]{:S(2)}, u32[]{:S(2)}) collective-permute-start(bf16[2,256,128]{1,2,0:T(8,128)(2,1)S(1)} %broadcast_select_fusion.5), channel_id=1, source_target_pairs={{8,0},{16,8},{24,16},{32,24},{40,32},{48,40},{56,48},{64,56},{72,6... | collective-permute-start | bytes 393224 | tf_op jit(solution)/shard_map/ppermute | solution.py:21
  148.6 9.0 %collective-permute-start.3 = (bf16[2,256,128]{1,2,0:T(8,128)(2,1)S(1)}, bf16[2,256,128]{1,2,0:T(8,128)(2,1)S(1)}, u32[]{:S(2)}, u32[]{:S(2)}) collective-permute-start(bf16[2,256,128]{1,2,0:T(8,128)(2,1)S(1)} %collective-permute-done.2), channel_id=1, source_target_pairs={{0,8},{8,16},{16,24},{24,32},{32,40},{40,48},{48,56},{56,64},{64,7... | collective-permute-start | bytes 393224 | tf_op jit(solution)/shard_map/ppermute | solution.py:21
  157.6 14.1 %collective-permute-start.14 = (bf16[2,256,128]{1,2,0:T(8,128)(2,1)S(1)}, bf16[2,256,128]{1,2,0:T(8,128)(2,1)S(1)}, u32[]{:S(2)}, u32[]{:S(2)}) collective-permute-start(bf16[2,256,128]{1,2,0:T(8,128)(2,1)S(1)} %broadcast_select_fusion.4), channel_id=1, source_target_pairs={{8,0},{16,8},{24,16},{32,24},{40,32},{48,40},{56,48},{64,56},{72,6... | collective-permute-start | bytes 393224 | tf_op jit(solution)/shard_map/ppermute | solution.py:21
  162.7 9.0 %collective-permute-start.4 = (bf16[2,256,128]{1,2,0:T(8,128)(2,1)S(1)}, bf16[2,256,128]{1,2,0:T(8,128)(2,1)S(1)}, u32[]{:S(2)}, u32[]{:S(2)}) collective-permute-start(bf16[2,256,128]{1,2,0:T(8,128)(2,1)S(1)} %collective-permute-done.3), channel_id=1, source_target_pairs={{0,8},{8,16},{16,24},{24,32},{32,40},{40,48},{48,56},{56,64},{64,7... | collective-permute-start | bytes 393224 | tf_op jit(solution)/shard_map/ppermute | solution.py:21
  171.7 14.5 %collective-permute-start.15 = (bf16[2,256,128]{1,2,0:T(8,128)(2,1)S(1)}, bf16[2,256,128]{1,2,0:T(8,128)(2,1)S(1)}, u32[]{:S(2)}, u32[]{:S(2)}) collective-permute-start(bf16[2,256,128]{1,2,0:T(8,128)(2,1)S(1)} %broadcast_select_fusion.3), channel_id=1, source_target_pairs={{8,0},{16,8},{24,16},{32,24},{40,32},{48,40},{56,48},{64,56},{72,6... | collective-permute-start | bytes 393224 | tf_op jit(solution)/shard_map/ppermute | solution.py:21
  177.3 9.0 %collective-permute-start.5 = (bf16[2,256,128]{1,2,0:T(8,128)(2,1)S(1)}, bf16[2,256,128]{1,2,0:T(8,128)(2,1)S(1)}, u32[]{:S(2)}, u32[]{:S(2)}) collective-permute-start(bf16[2,256,128]{1,2,0:T(8,128)(2,1)S(1)} %collective-permute-done.4), channel_id=1, source_target_pairs={{0,8},{8,16},{16,24},{24,32},{32,40},{40,48},{48,56},{56,64},{64,7... | collective-permute-start | bytes 393224 | tf_op jit(solution)/shard_map/ppermute | solution.py:21
  186.3 14.1 %collective-permute-start.16 = (bf16[2,256,128]{1,2,0:T(8,128)(2,1)S(1)}, bf16[2,256,128]{1,2,0:T(8,128)(2,1)S(1)}, u32[]{:S(2)}, u32[]{:S(2)}) collective-permute-start(bf16[2,256,128]{1,2,0:T(8,128)(2,1)S(1)} %broadcast_select_fusion.2), channel_id=1, source_target_pairs={{8,0},{16,8},{24,16},{32,24},{40,32},{48,40},{56,48},{64,56},{72,6... | collective-permute-start | bytes 393224 | tf_op jit(solution)/shard_map/ppermute | solution.py:21
  191.4 9.0 %collective-permute-start.6 = (bf16[2,256,128]{1,2,0:T(8,128)(2,1)S(1)}, bf16[2,256,128]{1,2,0:T(8,128)(2,1)S(1)}, u32[]{:S(2)}, u32[]{:S(2)}) collective-permute-start(bf16[2,256,128]{1,2,0:T(8,128)(2,1)S(1)} %collective-permute-done.5), channel_id=1, source_target_pairs={{0,8},{8,16},{16,24},{24,32},{32,40},{40,48},{48,56},{56,64},{64,7... | collective-permute-start | bytes 393224 | tf_op jit(solution)/shard_map/ppermute | solution.py:21
  201.0 11.3 %collective-permute-start.17 = (bf16[2,256,128]{1,2,0:T(8,128)(2,1)}, bf16[2,256,128]{1,2,0:T(8,128)(2,1)S(1)}, u32[]{:S(2)}, u32[]{:S(2)}) collective-permute-start(bf16[2,256,128]{1,2,0:T(8,128)(2,1)} %broadcast_select_fusion.1), channel_id=1, source_target_pairs={{8,0},{16,8},{24,16},{32,24},{40,32},{48,40},{56,48},{64,56},{72,6... | collective-permute-start | bytes 393224 | tf_op jit(solution)/shard_map/ppermute | solution.py:21
  203.0 9.3 %collective-permute-start.7 = (bf16[2,256,128]{1,2,0:T(8,128)(2,1)S(1)}, bf16[2,256,128]{1,2,0:T(8,128)(2,1)S(1)}, u32[]{:S(2)}, u32[]{:S(2)}) collective-permute-start(bf16[2,256,128]{1,2,0:T(8,128)(2,1)S(1)} %collective-permute-done.6), channel_id=1, source_target_pairs={{0,8},{8,16},{16,24},{24,32},{32,40},{40,48},{48,56},{56,64},{64,7... | collective-permute-start | bytes 393224 | tf_op jit(solution)/shard_map/ppermute | solution.py:21
  212.5 9.0 %collective-permute-start.8 = (bf16[2,256,128]{1,2,0:T(8,128)(2,1)S(1)}, bf16[2,256,128]{1,2,0:T(8,128)(2,1)S(1)}, u32[]{:S(2)}, u32[]{:S(2)}) collective-permute-start(bf16[2,256,128]{1,2,0:T(8,128)(2,1)S(1)} %collective-permute-done.7), channel_id=1, source_target_pairs={{0,8},{8,16},{16,24},{24,32},{32,40},{40,48},{48,56},{56,64},{64,7... | collective-permute-start | bytes 393224 | tf_op jit(solution)/shard_map/ppermute | solution.py:21
  226.9 58.8 %copy-start.1 = (bf16[4096,128]{1,0:T(8,128)(2,1)S(1)}, bf16[4096,128]{1,0:T(8,128)(2,1)}, u32[]{:S(2)}) copy-start(bf16[4096,128]{1,0:T(8,128)(2,1)} %param.53) | copy-start | bytes 3145732
where the time goes:
time: 291 us; the launch traced here: 286 us
  other arithmetic  57.2 us (20%)
  starting transfers between devices  55.6 us (19%)
  blocking collectives  55 us (19%)
  local copies, waits for them, and re-layouts  44.8 us (15%)
  matrix products  29.8 us (10%)
  waiting for transfers between devices  28.4 us (10%)
  between operations  13.8 us (5%)
    ppermute x18, starting transfers between devices, passed_along(): return lax.ppermute(shard, axis, pairs)  55.6 us
    all_to_all x1, blocking collectives, summed_on_arrival(): lax.all_to_all(pieces, axis, split_axis=0, concat_axis=0, tiled=True)  55 us
    ppermute x18, waiting for transfers between devices, passed_along(): return lax.ppermute(shard, axis, pairs)  28.4 us
    gather x9, local copies, waits for them, and re-layouts, shards(): jnp.take(doc_ids, jnp.maximum(upper_kpos, 0))  15.5 us
    gather x9, local copies, waits for them, and re-layouts, shards(): jnp.take(doc_ids, jnp.maximum(lower_kpos, 0))  15.5 us
    add x15, other arithmetic, update(): weight_sum = weight_sum * factor + jnp.sum(weights, axis=-1)  10.4 us
    dot_general x15, matrix products, update(): jnp.einsum('kgts,skd->tkgd', weights.astype(jnp.bfloat16), value_heads, p...  9.1 us
    mul x13, other arithmetic, update(): accumulated * jnp.transpose(factor, (2, 0, 1))[..., None] + added  8.89 us
  transfers between devices with their start and end apart: 18, of which 8 were waited for; matrix products, arithmetic and copies ran while one was open for 39% of the time, Pallas kernels for 0%

commit v1 on v0

v1 whole, which is shorter than its diff:
```python
import math

import jax
import jax.numpy as jnp
import numpy as np
from jax import lax
from jax.experimental import pallas as pl
from jax.experimental.pallas import tpu as pltpu
from jax.sharding import PartitionSpec as P

D = 4096
HEADS = 32
HD = 128
GROUP = 4
STRETCH = 256
N_CP = 16
REACH = 9
CHUNK = 512
N_CHUNK = D // CHUNK
NEG = -1e30
EPS = 1e-05
THETA = 500000.0
QSCALE = math.log2(math.e) / math.sqrt(HD)
ONES = 16
F32 = jnp.float32
BF16 = jnp.bfloat16


def rope_tables():
    half = HD // 2
    freqs = THETA ** (-2.0 * np.arange(half) / HD)
    inner = np.arange(STRETCH)[:, None] * freqs[None, :]
    outer = (np.arange(2 * N_CP) * STRETCH)[:, None] * freqs[None, :]

    def both(angles):
        c, s = np.cos(angles), np.sin(angles)
        return np.stack([np.concatenate([c, c], 1), np.concatenate([s, s], 1)])

    return both(inner).astype(np.float32), both(outer).astype(np.float32)


def kernel(
    tokens, gain, wq, wk, wv, wo, docs, rope_in, rope_out, out,
    x, xg, wkv, wqv, wo_own, wo_sib, acckv, accq, ssq, kvbuf, qs,
    m_ref, acc_ref, attn_own, attn_sib, send_a, recv_a, send_b, recv_b, qstart,
    in_sems, wq_sems, wo_sems, wos_send, wos_recv, kv_send, kv_recv,
    at_send, at_recv, a_send, a_recv, b_send, b_recv,
):
    d = lax.axis_index("cp")
    t = lax.axis_index("tp")
    z, core = t // 2, t % 2
    sib = t + 1 - 2 * core
    t_up = lax.rem(z + 1, 4) * 2 + core
    t_dn = lax.rem(z + 3, 4) * 2 + core
    zs = [z, lax.rem(z + 1, 4), lax.rem(z + 3, 4), lax.rem(z + 2, 4)]
    cl, cu = d, 2 * N_CP - 1 - d

    def in_copies(i):
        rows = pl.ds(i * CHUNK, CHUNK)
        return (
            pltpu.make_async_copy(tokens.at[:, rows], x.at[:, rows], in_sems.at[0, i]),
            pltpu.make_async_copy(wk.at[rows, :], wkv.at[rows, 0:HD], in_sems.at[1, i]),
            pltpu.make_async_copy(wv.at[rows, :], wkv.at[rows, HD : 2 * HD], in_sems.at[2, i]),
        )

    def wq_copy(i):
        rows = pl.ds(i * CHUNK, CHUNK)
        return pltpu.make_async_copy(wq.at[rows, :], wqv.at[rows, :], wq_sems.at[i])

    def wo_copy(i):
        cols = pl.ds(pl.multiple_of((2 * i + core) * 512, 512), 512)
        return pltpu.make_async_copy(wo.at[:, cols], wo_own.at[i], wo_sems.at[i])

    for i in range(N_CHUNK):
        for c in in_copies(i):
            c.start()

    barrier = pltpu.get_barrier_semaphore()
    for r in range(1, N_CP):
        pl.semaphore_signal(barrier, 1, device_id={"cp": lax.rem(d + r, N_CP), "tp": t})
    for other in (sib, t_up, t_dn):
        pl.semaphore_signal(barrier, 1, device_id={"cp": d, "tp": other})

    for i in range(N_CHUNK):
        wq_copy(i).start()
    for i in range(4):
        wo_copy(i).start()

    table = docs[...]
    rows = [docs[pl.ds(cl, 1), :], docs[pl.ds(cu, 1), :]]
    starts = [jnp.zeros((1, STRETCH), F32) for _ in rows]
    for v in range(1, 16):
        below = jnp.where(table < v, 1.0, 0.0)
        count = jnp.sum(jnp.sum(below, axis=0, keepdims=True), axis=1, keepdims=True)
        starts = [jnp.where(r >= v, count, s) for r, s in zip(rows, starts)]
    qstart[0:1, :] = starts[0].astype(jnp.int32)
    qstart[1:2, :] = starts[1].astype(jnp.int32)

    acckv[...] = jnp.zeros_like(acckv)
    ssq[...] = jnp.zeros_like(ssq)

    def kv_step(i, carry):
        for c in in_copies(i):
            c.wait()
        cols = pl.ds(pl.multiple_of(i * CHUNK, CHUNK), CHUNK)
        xf = x[:, cols].astype(F32)
        sq = xf * xf
        ssq[...] += sq[:, 0:128] + sq[:, 128:256] + sq[:, 256:384] + sq[:, 384:512]
        scaled = (xf * gain[:, cols].astype(F32)).astype(BF16)
        xg[:, cols] = scaled
        acckv[...] += jnp.dot(scaled, wkv[cols, :], preferred_element_type=F32)
        return carry

    lax.fori_loop(0, N_CHUNK, kv_step, 0)
    mean = jnp.sum(ssq[...], axis=1, keepdims=True) * (1.0 / D)
    factor = lax.rsqrt(mean + EPS)
    ssq[...] = jnp.broadcast_to(factor, (2 * STRETCH, HD))

    sign = jnp.where(lax.broadcasted_iota(jnp.int32, (1, HD), 1) < HD // 2, -1.0, 1.0)

    def rope(h):
        c = cl if h == 0 else cu
        co, so = rope_out[0, pl.ds(c, 1), :], rope_out[1, pl.ds(c, 1), :]
        ci, si = rope_in[0], rope_in[1]
        return ci * co - si * so, (ci * so + si * co) * sign

    for h, c in ((0, cl), (1, cu)):
        rs = slice(h * STRETCH, (h + 1) * STRETCH)
        cosine, sine = rope(h)
        kf = acckv[rs, 0:HD] * ssq[rs, :]
        kvbuf[c, 0:STRETCH, :] = (kf * cosine + pltpu.roll(kf, HD // 2, 1) * sine).astype(BF16)
        vf = acckv[rs, HD : 2 * HD] * ssq[rs, :]
        kvbuf[c, STRETCH : STRETCH + HD, :] = vf[0:HD, :].T.astype(BF16)
        kvbuf[c, STRETCH + HD : STRETCH + 2 * HD, :] = vf[HD : 2 * HD, :].T.astype(BF16)

    pl.semaphore_wait(barrier, N_CP - 1 + 3)

    def kv_copy(c, e, s):
        return pltpu.make_async_remote_copy(
            src_ref=kvbuf.at[c], dst_ref=kvbuf.at[c], send_sem=kv_send.at[s],
            recv_sem=kv_recv.at[c], device_id={"cp": e, "tp": t},
        )

    def kv_sends(act):
        for r in range(1, REACH + 1):
            @pl.when(d + r < N_CP)
            def _():
                act(kv_copy(cl, d + r, r - 1))
        for r in range(1, REACH + 1):
            @pl.when(d - r >= 0)
            def _():
                act(kv_copy(cu, d - r, REACH + r - 1))
        for r in range(1, N_CP):
            e = lax.rem(d + r, N_CP)
            direct = (d + r < N_CP) & (r <= REACH)
            @pl.when((e >= 22 - d) & (e <= 30 - d) & jnp.logical_not(direct))
            def _():
                act(kv_copy(cl, e, 2 * REACH + r - 1))

    kv_sends(lambda c: c.start())

    def wos_copy(i):
        cols = pl.ds(pl.multiple_of((2 * i + 1 - core) * 512, 512), 512)
        return pltpu.make_async_remote_copy(
            src_ref=wo.at[:, cols], dst_ref=wo_sib.at[i], send_sem=wos_send.at[i],
            recv_sem=wos_recv.at[i], device_id={"cp": d, "tp": sib},
        )

    for i in range(4):
        wos_copy(i).start()

    accq[...] = jnp.zeros_like(accq)

    def q_step(i, carry):
        wq_copy(i).wait()
        cols = pl.ds(pl.multiple_of(i * CHUNK, CHUNK), CHUNK)
        accq[...] += jnp.dot(xg[:, cols], wqv[cols, :], preferred_element_type=F32)
        return carry

    lax.fori_loop(0, N_CHUNK, q_step, 0)
    for h in range(2):
        rs = slice(h * STRETCH, (h + 1) * STRETCH)
        cosine, sine = rope(h)
        scale = ssq[rs, :] * QSCALE
        for g in range(GROUP):
            qf = accq[rs, g * HD : (g + 1) * HD] * scale
            qs[h, g * STRETCH : (g + 1) * STRETCH, :] = (
                qf * cosine + pltpu.roll(qf, HD // 2, 1) * sine
            ).astype(BF16)

    key_row = lax.broadcasted_iota(jnp.int32, (STRETCH, STRETCH), 0)
    query_col = lax.broadcasted_iota(jnp.int32, (STRETCH, STRETCH), 1)
    ones = jnp.ones((ONES, STRETCH), BF16)

    def block(h, s, first):
        keys = kvbuf[s, 0:STRETCH, :]
        vt = jnp.concatenate(
            [kvbuf[s, STRETCH : STRETCH + HD, :], kvbuf[s, STRETCH + HD : STRETCH + 2 * HD, :]], axis=1
        )
        vt = jnp.concatenate([vt, ones], axis=0)
        mask = key_row >= qstart[h : h + 1, :] - s * STRETCH
        if first:
            mask = mask & (key_row <= query_col)
        for g in range(GROUP):
            q = qs[h, g * STRETCH : (g + 1) * STRETCH, :]
            scores = lax.dot_general(keys, q, (((1,), (1,)), ((), ())), preferred_element_type=F32)
            scores = jnp.where(mask, scores, NEG)
            top = jnp.max(scores, axis=0, keepdims=True)
            if not first:
                before = m_ref[h, g : g + 1, :]
                top = jnp.maximum(top, before)
            weights = jnp.exp2(scores - top).astype(BF16)
            added = jnp.dot(vt, weights, preferred_element_type=F32)
            if first:
                acc_ref[h, g] = added
            else:
                acc_ref[h, g] = acc_ref[h, g] * jnp.exp2(before - top) + added
            m_ref[h, g : g + 1, :] = top

    def finish(h):
        for g in range(GROUP):
            o = acc_ref[h, g, 0:HD, :] / acc_ref[h, g, HD : HD + 1, :]
            attn_own[h, :, g * HD : (g + 1) * HD] = o.T.astype(BF16)

    def kv_wait(s):
        kv_copy(s, d, 0).wait_recv()

    def lower_step(k, carry):
        @pl.when(cl >= k)
        def _():
            kv_wait(cl - k)
            block(0, cl - k, False)
        return carry

    def upper_step(k, carry):
        s = cu - k
        @pl.when((s != d) & ((s > d) | (s < d - REACH)))
        def _():
            kv_wait(s)
        block(1, s, False)
        return carry

    def at_copy(h):
        return pltpu.make_async_remote_copy(
            src_ref=attn_own.at[h], dst_ref=attn_sib.at[h], send_sem=at_send.at[h],
            recv_sem=at_recv.at[h], device_id={"cp": d, "tp": sib},
        )

    def project(h, i):
        zz = zs[i]
        return jnp.dot(attn_own[h], wo_own[zz], preferred_element_type=F32) + jnp.dot(
            attn_sib[h], wo_sib[zz], preferred_element_type=F32
        )

    def a_copy(h, way):
        return pltpu.make_async_remote_copy(
            src_ref=send_a.at[h, way], dst_ref=recv_a.at[h, way], send_sem=a_send.at[h, way],
            recv_sem=a_recv.at[h, way], device_id={"cp": d, "tp": t_up if way == 0 else t_dn},
        )

    def b_copy(h, way, piece):
        return pltpu.make_async_remote_copy(
            src_ref=send_b.at[h, way, piece], dst_ref=recv_b.at[h, way, piece],
            send_sem=b_send.at[h, way, piece], recv_sem=b_recv.at[h, way, piece],
            device_id={"cp": d, "tp": t_up if way == 0 else t_dn},
        )

    summed = [slice(0, 256), slice(256, 512)]
    plain = [slice(256, 512), slice(0, 256)]
    held = [None, None]

    def scatter_first(h):
        at_copy(h).wait_recv()
        far = project(h, 3)
        for way in range(2):
            send_a[h, way] = far[:, summed[way]].astype(BF16)
            a_copy(h, way).start()
        for way in range(2):
            near = project(h, 1 + way)
            acckv_like = near[:, summed[way]]
            accq[h * STRETCH : (h + 1) * STRETCH, way * 256 : (way + 1) * 256] = acckv_like
            send_b[h, way, 1] = near[:, plain[way]].astype(BF16)
            b_copy(h, way, 1).start()

    def scatter_second(h):
        for way in range(2):
            a_copy(h, way).wait_recv()
            own = accq[h * STRETCH : (h + 1) * STRETCH, way * 256 : (way + 1) * 256]
            send_b[h, way, 0] = (own + recv_a[h, way].astype(F32)).astype(BF16)
            b_copy(h, way, 0).start()

    def scatter_last(h):
        mine = project(h, 0)
        for way in range(2):
            for piece in range(2):
                b_copy(h, way, piece).wait_recv()
        rs = slice(h * STRETCH, (h + 1) * STRETCH)
        out[rs, 0:256] = (
            mine[:, 0:256] + recv_b[h, 0, 0].astype(F32) + recv_b[h, 1, 1].astype(F32)
        ).astype(BF16)
        out[rs, 256:512] = (
            mine[:, 256:512] + recv_b[h, 0, 1].astype(F32) + recv_b[h, 1, 0].astype(F32)
        ).astype(BF16)

    block(0, cl, True)
    block(1, cu, True)
    lax.fori_loop(1, REACH + 1, lower_step, 0)
    finish(0)
    at_copy(0).start()
    for i in range(4):
        wo_copy(i).wait()
        wos_copy(i).wait_recv()
    lax.fori_loop(1, 3, upper_step, 0)
    scatter_first(0)
    lax.fori_loop(3, 7, upper_step, 0)
    scatter_second(0)
    lax.fori_loop(7, REACH + 1, upper_step, 0)
    finish(1)
    at_copy(1).start()
    scatter_last(0)
    scatter_first(1)
    scatter_second(1)
    scatter_last(1)

    kv_sends(lambda c: c.wait_send())
    for i in range(4):
        wos_copy(i).wait_send()
    for h in range(2):
        at_copy(h).wait_send()
        for way in range(2):
            a_copy(h, way).wait_send()
            for piece in range(2):
                b_copy(h, way, piece).wait_send()


def step(tokens, gain, w_query, w_key, w_value, w_out, doc_ids):
    rope_in, rope_out = rope_tables()
    any_space = pl.BlockSpec(memory_space=pl.ANY)
    vmem = pl.BlockSpec(memory_space=pltpu.VMEM)
    rows = 2 * STRETCH
    dma = pltpu.SemaphoreType.DMA
    return pl.pallas_call(
        kernel,
        out_shape=jax.ShapeDtypeStruct((rows, 512), BF16),
        in_specs=[any_space, vmem, any_space, any_space, any_space, any_space, vmem, vmem, vmem],
        out_specs=vmem,
        scratch_shapes=[
            pltpu.VMEM((rows, D), BF16),
            pltpu.VMEM((rows, D), BF16),
            pltpu.VMEM((D, 2 * HD), BF16),
            pltpu.VMEM((D, GROUP * HD), BF16),
            pltpu.VMEM((4, 512, 512), BF16),
            pltpu.VMEM((4, 512, 512), BF16),
            pltpu.VMEM((rows, 2 * HD), F32),
            pltpu.VMEM((rows, GROUP * HD), F32),
            pltpu.VMEM((rows, HD), F32),
            pltpu.VMEM((2 * N_CP, 2 * STRETCH, HD), BF16),
            pltpu.VMEM((2, GROUP * STRETCH, HD), BF16),
            pltpu.VMEM((2, 8, STRETCH), F32),
            pltpu.VMEM((2, GROUP, HD + ONES, STRETCH), F32),
            pltpu.VMEM((2, STRETCH, 512), BF16),
            pltpu.VMEM((2, STRETCH, 512), BF16),
            pltpu.VMEM((2, 2, STRETCH, 256), BF16),
            pltpu.VMEM((2, 2, STRETCH, 256), BF16),
            pltpu.VMEM((2, 2, 2, STRETCH, 256), BF16),
            pltpu.VMEM((2, 2, 2, STRETCH, 256), BF16),
            pltpu.VMEM((8, STRETCH), jnp.int32),
            dma((3, N_CHUNK)),
            dma((N_CHUNK,)),
            dma((4,)),
            dma((4,)),
            dma((4,)),
            dma((2 * REACH + N_CP - 1,)),
            dma((2 * N_CP,)),
            dma((2,)),
            dma((2,)),
            dma((2, 2)),
            dma((2, 2)),
            dma((2, 2, 2)),
            dma((2, 2, 2)),
        ],
        compiler_params=pltpu.CompilerParams(
            collective_id=0, has_side_effects=True, vmem_limit_bytes=60 * 1024 * 1024
        ),
        name="block",
    )(
        tokens, gain.reshape(1, D), w_query, w_key, w_value, w_out,
        doc_ids.reshape(2 * N_CP, STRETCH), jnp.asarray(rope_in), jnp.asarray(rope_out),
    )


def solution(mesh):
    in_specs = (P("cp", None), P(), P(None, "tp"), P(None, "tp"), P(None, "tp"), P("tp", None), P())
    return jax.shard_map(step, mesh=mesh, in_specs=in_specs, out_specs=P("cp", "tp"), check_vma=False)
```

time: 291 us -> 78.6 us (0.27)
  the two profiles are of different devices: /device:TPU:16 before, /device:TPU:29 now
where the time goes in v1:
time: 78.6 us; the launch traced here: 78.4 us
  Pallas kernels  73.8 us (94%)
  local copies, waits for them, and re-layouts  4.55 us (6%)
    pallas_call x1, Pallas kernels, step(): pl.pallas_call(kernel, out_shape=jax.ShapeDtypeStruct((rows, 512), BF16),...  73.8 us
    unnamed x1, local copies, waits for them, and re-layouts  1.87 us

profile of v1, /device:TPU:29, one launch (start us, length us, event | category | flops | bytes accessed | tf_op | source)
XLA Modules:
  0.0 78.4 jit_solution(8742956726449145873)
XLA Ops:
  0.0 1.3 %reshape.6.gain = bf16[1,4096]{1,0:T(2,128)(2,1)} reshape(bf16[4096]{0:T(1024)(128)(2,1)} %param.10) | data formatting | bytes 16384 | tf_op jit(solution)/shard_map/reshape | solution.py:387
  1.3 1.4 %reshape.7.docs = s32[32,256]{1,0:T(8,128)} reshape(s32[8192]{0:T(1024)} %param.15) | data formatting | bytes 65536 | tf_op jit(solution)/shard_map/reshape | solution.py:388
  2.7 73.8 %block.1 = bf16[512,512]{1,0:T(8,128)(2,1)} custom-call(bf16[512,4096]{1,0:T(8,128)(2,1)} %tokens.1, bf16[1,4096]{1,0:T(2,128)(2,1)} %reshape.6.gain, bf16[4096,512]{1,0:T(8,128)(2,1)} %wq.1, bf16[4096,128]{1,0:T(8,128)(2,1)} %wk.1, bf16[4096,128]{1,0:T(8,128)(2,1)} %wv.1, bf16[512,4096]{1,0:T(8,128)(2,1)} %wo.1, s32[32,256]{1,0:T(8,128)} %reshape.7.docs, ...), custom_call_target="tpu_custom_call" | custom-call | tf_op jit(solution)/shard_map/block/pallas_call | solution.py:342
  76.5 1.9 %copy.11 = bf16[512,512]{1,0:T(8,128)(2,1)} copy(bf16[512,512]{1,0:T(8,128)(2,1)} %block.1) | data formatting | bytes 1048576

commit v2 on v1

--- a/solution.py
+++ b/solution.py
@@ -25,6 +25,33 @@
 F32 = jnp.float32
 BF16 = jnp.bfloat16
 
+TABLE = [
+    [64, 385, 384, 65, 1271, 1081, 1084, 3318, 3128, 3133, 121, 1199, 1072, 1076, 111, 3246, 3121, 1082, 113, 3125, 3131, 180, 1459, 1069, 3122, 3244],
+    [322, 188, 323, 189, 1344, 1204, 1082, 3073, 3189, 3131, 186, 116, 187, 1069, 1075, 1079, 109, 179, 3116, 3122, 3126, 108, 178, 1080, 3129, 1066, 3115, 1135, 3118, 1072, 3121],
+    [68, 261, 186, 260, 69, 187, 1346, 1203, 1081, 3139, 3250, 3128, 114, 184, 1280, 3073, 1067, 235, 3114, 1072, 1077, 106, 176, 3121, 3124, 1064, 117, 3113, 1325, 1078, 109, 3116, 3127, 1071, 3118],
+    [262, 249, 263, 248, 1153, 1284, 1136, 3328, 3077, 3185, 176, 1282, 1192, 1079, 3331, 3113, 3254, 1074, 183, 1071, 1323, 3246, 3114, 1076, 3125, 1062, 3123, 1069, 3116, 3111],
+    [72, 393, 567, 392, 73, 566, 1473, 1583, 1072, 1076, 3328, 3822, 3121, 3125, 239, 565, 1026, 1286, 1062, 230, 3075, 3335, 1581, 173, 113, 3111, 1064, 3628, 258, 103, 172, 1284, 3077, 3113, 104, 1061, 1322, 3108, 3115, 1075, 3122],
+    [331, 692, 330, 693, 1410, 1096, 1581, 1074, 3523, 3081, 3628, 3123, 73, 172, 1024, 3073, 1285, 1578, 133, 108, 3332, 1060, 1582, 100, 170, 3109, 3115, 3119, 257, 101, 171, 1030, 1059, 1062, 178, 3079, 3106, 1073, 3111, 1065, 3120, 3112],
+    [268, 77, 178, 563, 76, 269, 562, 179, 1477, 1035, 1579, 1073, 3204, 3338, 3626, 3120, 75, 260, 74, 171, 561, 1026, 1030, 1032, 1065, 390, 553, 106, 3075, 3079, 1058, 391, 98, 3081, 3107, 3112, 1024, 99, 176, 3073, 1068, 1056, 1380, 1070, 3109, 3119, 3117, 3105, 1062, 3111],
+    [270, 624, 177, 271, 176, 625, 1222, 1033, 1293, 1576, 3271, 3080, 3084, 3625, 262, 263, 232, 1025, 1028, 3077, 1056, 129, 324, 3072, 1035, 1054, 1070, 174, 3082, 3103, 3119, 1026, 175, 1830, 1066, 3075, 166, 3105, 1058, 1069, 3107, 3623, 3116, 3115, 1060, 3109],
+    [144, 337, 559, 336, 145, 558, 1481, 1574, 1065, 1068, 3528, 3111, 3112, 3629, 102, 679, 1025, 1291, 1038, 1057, 139, 78, 553, 3072, 3082, 3343, 1061, 64, 677, 1054, 3103, 3108, 1286, 70, 676, 1036, 3085, 3104, 3335, 71, 1027, 1052, 3074, 284, 103, 1029, 3101, 1059, 3076, 3106, 1066, 3115],
+    [274, 83, 172, 557, 82, 275, 556, 173, 1483, 1041, 1061, 1578, 3466, 3152, 3620, 3115, 1051, 81, 164, 549, 1026, 1033, 1292, 1571, 66, 140, 3075, 3080, 3341, 3618, 195, 1062, 1065, 264, 1029, 1053, 133, 102, 553, 1038, 3100, 3076, 3098, 162, 101, 1024, 3087, 3073, 1055, 171, 1030, 3112, 3079, 1056, 3105, 3102, 3111],
+    [276, 85, 170, 555, 84, 277, 554, 171, 1484, 1043, 1058, 1577, 3469, 3090, 3107, 3112, 83, 546, 1052, 82, 547, 169, 1029, 1035, 1294, 3101, 69, 156, 3082, 3343, 1040, 1568, 74, 143, 3076, 3089, 1055, 267, 1050, 98, 168, 1026, 1030, 1033, 3617, 90, 160, 3075, 3079, 3080, 3230, 99, 1062, 3623, 1049, 1061, 3108, 3096, 3099],
+    [278, 552, 233, 279, 232, 553, 1486, 1040, 1045, 1568, 3535, 3089, 3092, 1566, 2070, 3743, 276, 94, 1033, 1036, 3085, 1052, 137, 333, 1030, 3080, 1043, 3617, 136, 275, 92, 3079, 3090, 1063, 3165, 679, 1028, 3077, 1035, 1049, 3082, 1573, 1179, 1058, 3108, 3110, 3096, 3098, 3107],
+    [88, 153, 550, 152, 89, 551, 1233, 1569, 1060, 3280, 1055, 3621, 2072, 1050, 3104, 607, 1033, 1170, 1046, 73, 544, 3080, 3091, 3095, 86, 1035, 1102, 1571, 3087, 3082, 3102, 79, 1044, 3093, 1030, 1036, 3085, 3079, 3099, 1053, 3100, 3106],
+    [90, 164, 549, 91, 548, 165, 154, 539, 1106, 1048, 1059, 146, 547, 3155, 3097, 3106, 2074, 147, 546, 1053, 88, 1035, 1041, 541, 163, 1044, 81, 3082, 3088, 138, 538, 3093, 74, 1055, 148, 543, 1036, 3100, 1033, 140, 3085, 1569, 1046, 157, 3080, 3104, 1038, 162, 3095, 3087, 3102],
+    [92, 546, 163, 93, 162, 547, 540, 157, 1044, 1114, 1056, 148, 541, 3093, 3163, 1054, 2076, 149, 544, 3105, 85, 1036, 1042, 538, 156, 1049, 76, 3085, 3091, 673, 1046, 3096, 542, 160, 1038, 3095, 1041, 151, 537, 3087, 3088, 1034, 536, 158, 3083, 3103],
+    [672, 97, 670, 95, 543, 96, 161, 1046, 1049, 1052, 86, 153, 540, 3095, 3096, 3101, 2078, 150, 87, 545, 1038, 1041, 1050, 78, 151, 541, 3087, 3088, 3099, 144, 537, 94, 1044, 3093, 85, 539, 159, 1036, 3085, 1042, 77, 536, 3091, 91],
+]
+MARKS = [
+    [4, 4, 6, 4, 6, 4, 8, 6, 6, 8, 8, 6, 6, 8, 8, 7],
+    [4, 7, 15, 14, 32, 35, 39, 35, 48, 52, 49, 40, 37, 49, 44, 42],
+    [10, 13, 21, 19, 37, 41, 44, 40, 51, 56, 54, 45, 41, 50, 45, 43],
+    [23, 29, 33, 27, 40, 41, 49, 45, 51, 56, 58, 48, 41, 50, 45, 43],
+    [26, 31, 35, 30, 41, 42, 50, 46, 52, 57, 59, 49, 42, 51, 46, 44],
+]
+ENTRIES = max(len(row) for row in TABLE)
+
 
 def rope_tables():
     half = HD // 2
@@ -54,6 +81,13 @@
     t_dn = lax.rem(z + 3, 4) * 2 + core
     zs = [z, lax.rem(z + 1, 4), lax.rem(z + 3, 4), lax.rem(z + 2, 4)]
     cl, cu = d, 2 * N_CP - 1 - d
+    px, py = lax.rem(d, 4), lax.div(d, 4)
+    beside = [
+        py * 4 + lax.rem(px + 1, 4),
+        py * 4 + lax.rem(px + 3, 4),
+        lax.rem(py + 1, 4) * 4 + px,
+        lax.rem(py + 3, 4) * 4 + px,
+    ]
 
     def in_copies(i):
         rows = pl.ds(i * CHUNK, CHUNK)
@@ -76,15 +110,36 @@
             c.start()
 
     barrier = pltpu.get_barrier_semaphore()
-    for r in range(1, N_CP):
-        pl.semaphore_signal(barrier, 1, device_id={"cp": lax.rem(d + r, N_CP), "tp": t})
+    for e in beside:
+        pl.semaphore_signal(barrier, 1, device_id={"cp": e, "tp": t})
     for other in (sib, t_up, t_dn):
         pl.semaphore_signal(barrier, 1, device_id={"cp": d, "tp": other})
 
-    for i in range(N_CHUNK):
-        wq_copy(i).start()
-    for i in range(4):
-        wo_copy(i).start()
+    here = [(d == e).astype(jnp.int32) for e in range(N_CP)]
+
+    def pick(values):
+        total = jnp.int32(0)
+        for e, v in enumerate(values):
+            if v:
+                total = total + here[e] * v
+        return total
+
+    def entry_of(row, i):
+        return row[i] if i < len(row) else 0
+
+    words = [
+        pick([entry_of(row, i) + 4096 * entry_of(row, i + 1) for row in TABLE])
+        for i in range(0, ENTRIES, 2)
+    ]
+
+    def entry(i):
+        j = lax.div(i, 2)
+        word = jnp.int32(0)
+        for k, w in enumerate(words):
+            word = jnp.where(j == k, w, word)
+        return jnp.where(lax.rem(i, 2) == 0, lax.rem(word, 4096), lax.div(word, 4096))
+
+    at_query, at_whole, at_first, at_second, n_entries = [pick(m) for m in MARKS]
 
     table = docs[...]
     rows = [docs[pl.ds(cl, 1), :], docs[pl.ds(cu, 1), :]]
@@ -95,6 +150,8 @@
         starts = [jnp.where(r >= v, count, s) for r, s in zip(rows, starts)]
     qstart[0:1, :] = starts[0].astype(jnp.int32)
     qstart[1:2, :] = starts[1].astype(jnp.int32)
+    m_ref[...] = jnp.full_like(m_ref, NEG)
+    acc_ref[...] = jnp.zeros_like(acc_ref)
 
     acckv[...] = jnp.zeros_like(acckv)
     ssq[...] = jnp.zeros_like(ssq)
@@ -102,6 +159,7 @@
     def kv_step(i, carry):
         for c in in_copies(i):
             c.wait()
+        wq_copy(i).start()
         cols = pl.ds(pl.multiple_of(i * CHUNK, CHUNK), CHUNK)
         xf = x[:, cols].astype(F32)
         sq = xf * xf
@@ -112,6 +170,8 @@
         return carry
 
     lax.fori_loop(0, N_CHUNK, kv_step, 0)
+    for i in range(4):
+        wo_copy(i).start()
     mean = jnp.sum(ssq[...], axis=1, keepdims=True) * (1.0 / D)
     factor = lax.rsqrt(mean + EPS)
     ssq[...] = jnp.broadcast_to(factor, (2 * STRETCH, HD))
@@ -128,36 +188,31 @@
         rs = slice(h * STRETCH, (h + 1) * STRETCH)
         cosine, sine = rope(h)
         kf = acckv[rs, 0:HD] * ssq[rs, :]
-        kvbuf[c, 0:STRETCH, :] = (kf * cosine + pltpu.roll(kf, HD // 2, 1) * sine).astype(BF16)
+        kvbuf[2 * c] = (kf * cosine + pltpu.roll(kf, HD // 2, 1) * sine).astype(BF16)
         vf = acckv[rs, HD : 2 * HD] * ssq[rs, :]
-        kvbuf[c, STRETCH : STRETCH + HD, :] = vf[0:HD, :].T.astype(BF16)
-        kvbuf[c, STRETCH + HD : STRETCH + 2 * HD, :] = vf[HD : 2 * HD, :].T.astype(BF16)
-
-    pl.semaphore_wait(barrier, N_CP - 1 + 3)
-
-    def kv_copy(c, e, s):
+        kvbuf[2 * c + 1, 0:HD, :] = vf[0:HD, :].T.astype(BF16)
+        kvbuf[2 * c + 1, HD : 2 * HD, :] = vf[HD : 2 * HD, :].T.astype(BF16)
+
+    pl.semaphore_wait(barrier, 7)
+
+    def kv_copy(p, way):
         return pltpu.make_async_remote_copy(
-            src_ref=kvbuf.at[c], dst_ref=kvbuf.at[c], send_sem=kv_send.at[s],
-            recv_sem=kv_recv.at[c], device_id={"cp": e, "tp": t},
-        )
-
-    def kv_sends(act):
-        for r in range(1, REACH + 1):
-            @pl.when(d + r < N_CP)
+            src_ref=kvbuf.at[p], dst_ref=kvbuf.at[p], send_sem=kv_send.at[way, p],
+            recv_sem=kv_recv.at[p], device_id={"cp": beside[way], "tp": t},
+        )
+
+    def pass_on(e, act):
+        p, ways = lax.rem(e, 64), lax.rem(lax.div(e, 64), 16)
+        for way in range(4):
+            @pl.when(lax.rem(lax.div(ways, 2**way), 2) == 1)
             def _():
-                act(kv_copy(cl, d + r, r - 1))
-        for r in range(1, REACH + 1):
-            @pl.when(d - r >= 0)
-            def _():
-                act(kv_copy(cu, d - r, REACH + r - 1))
-        for r in range(1, N_CP):
-            e = lax.rem(d + r, N_CP)
-            direct = (d + r < N_CP) & (r <= REACH)
-            @pl.when((e >= 22 - d) & (e <= 30 - d) & jnp.logical_not(direct))
-            def _():
-                act(kv_copy(cl, e, 2 * REACH + r - 1))
-
-    kv_sends(lambda c: c.start())
+                act(kv_copy(p, way))
+
+    def send_only(i, carry):
+        pass_on(entry(i), lambda c: c.start())
+        return carry
+
+    lax.fori_loop(0, at_query, send_only, 0)
 
     def wos_copy(i):
         cols = pl.ds(pl.multiple_of((2 * i + 1 - core) * 512, 512), 512)
@@ -169,15 +224,15 @@
     for i in range(4):
         wos_copy(i).start()
 
-    accq[...] = jnp.zeros_like(accq)
+    for i in range(N_CHUNK):
+        wq_copy(i).wait()
 
     def q_step(i, carry):
-        wq_copy(i).wait()
-        cols = pl.ds(pl.multiple_of(i * CHUNK, CHUNK), CHUNK)
-        accq[...] += jnp.dot(xg[:, cols], wqv[cols, :], preferred_element_type=F32)
+        cols = pl.ds(pl.multiple_of(i * 256, 256), 256)
+        accq[:, cols] = jnp.dot(xg[...], wqv[:, cols], preferred_element_type=F32)
         return carry
 
-    lax.fori_loop(0, N_CHUNK, q_step, 0)
+    lax.fori_loop(0, 2, q_step, 0)
     for h in range(2):
         rs = slice(h * STRETCH, (h + 1) * STRETCH)
         cosine, sine = rope(h)
@@ -192,53 +247,37 @@
     query_col = lax.broadcasted_iota(jnp.int32, (STRETCH, STRETCH), 1)
     ones = jnp.ones((ONES, STRETCH), BF16)
 
-    def block(h, s, first):
-        keys = kvbuf[s, 0:STRETCH, :]
-        vt = jnp.concatenate(
-            [kvbuf[s, STRETCH : STRETCH + HD, :], kvbuf[s, STRETCH + HD : STRETCH + 2 * HD, :]], axis=1
-        )
+    def block(h, s, own):
+        keys = kvbuf[2 * s]
+        vt = jnp.concatenate([kvbuf[2 * s + 1, 0:HD, :], kvbuf[2 * s + 1, HD : 2 * HD, :]], axis=1)
         vt = jnp.concatenate([vt, ones], axis=0)
         mask = key_row >= qstart[h : h + 1, :] - s * STRETCH
-        if first:
+        if own:
             mask = mask & (key_row <= query_col)
+        scores = [
+            lax.dot_general(
+                keys, qs[h, g * STRETCH : (g + 1) * STRETCH, :], (((1,), (1,)), ((), ())),
+                preferred_element_type=F32,
+            )
+            for g in range(GROUP)
+        ]
+        before = [m_ref[h, g : g + 1, :] for g in range(GROUP)]
+        held = [acc_ref[h, g] for g in range(GROUP)]
+        tops, added = [], []
         for g in range(GROUP):
-            q = qs[h, g * STRETCH : (g + 1) * STRETCH, :]
-            scores = lax.dot_general(keys, q, (((1,), (1,)), ((), ())), preferred_element_type=F32)
-            scores = jnp.where(mask, scores, NEG)
-            top = jnp.max(scores, axis=0, keepdims=True)
-            if not first:
-                before = m_ref[h, g : g + 1, :]
-                top = jnp.maximum(top, before)
-            weights = jnp.exp2(scores - top).astype(BF16)
-            added = jnp.dot(vt, weights, preferred_element_type=F32)
-            if first:
-                acc_ref[h, g] = added
-            else:
-                acc_ref[h, g] = acc_ref[h, g] * jnp.exp2(before - top) + added
-            m_ref[h, g : g + 1, :] = top
+            sc = jnp.where(mask, scores[g], NEG)
+            top = jnp.maximum(jnp.max(sc, axis=0, keepdims=True), before[g])
+            weights = jnp.exp2(sc - top).astype(BF16)
+            tops.append(top)
+            added.append(jnp.dot(vt, weights, preferred_element_type=F32))
+        for g in range(GROUP):
+            acc_ref[h, g] = held[g] * jnp.exp2(before[g] - tops[g]) + added[g]
+            m_ref[h, g : g + 1, :] = tops[g]
 
     def finish(h):
         for g in range(GROUP):
             o = acc_ref[h, g, 0:HD, :] / acc_ref[h, g, HD : HD + 1, :]
             attn_own[h, :, g * HD : (g + 1) * HD] = o.T.astype(BF16)
-
-    def kv_wait(s):
-        kv_copy(s, d, 0).wait_recv()
-
-    def lower_step(k, carry):
-        @pl.when(cl >= k)
-        def _():
-            kv_wait(cl - k)
-            block(0, cl - k, False)
-        return carry
-
-    def upper_step(k, carry):
-        s = cu - k
-        @pl.when((s != d) & ((s > d) | (s < d - REACH)))
-        def _():
-            kv_wait(s)
-        block(1, s, False)
-        return carry
 
     def at_copy(h):
         return pltpu.make_async_remote_copy(
@@ -267,7 +306,6 @@
 
     summed = [slice(0, 256), slice(256, 512)]
     plain = [slice(256, 512), slice(0, 256)]
-    held = [None, None]
 
     def scatter_first(h):
         at_copy(h).wait_recv()
@@ -277,8 +315,7 @@
             a_copy(h, way).start()
         for way in range(2):
             near = project(h, 1 + way)
-            acckv_like = near[:, summed[way]]
-            accq[h * STRETCH : (h + 1) * STRETCH, way * 256 : (way + 1) * 256] = acckv_like
+            accq[h * STRETCH : (h + 1) * STRETCH, way * 256 : (way + 1) * 256] = near[:, summed[way]]
             send_b[h, way, 1] = near[:, plain[way]].astype(BF16)
             b_copy(h, way, 1).start()
 
@@ -289,44 +326,82 @@
             send_b[h, way, 0] = (own + recv_a[h, way].astype(F32)).astype(BF16)
             b_copy(h, way, 0).start()
 
+    def scatter_mine(h):
+        accq[h * STRETCH : (h + 1) * STRETCH, :] = project(h, 0)
+
     def scatter_last(h):
-        mine = project(h, 0)
-        for way in range(2):
-            for piece in range(2):
+        rs = slice(h * STRETCH, (h + 1) * STRETCH)
+        for piece in (1, 0):
+            for way in range(2):
                 b_copy(h, way, piece).wait_recv()
-        rs = slice(h * STRETCH, (h + 1) * STRETCH)
         out[rs, 0:256] = (
-            mine[:, 0:256] + recv_b[h, 0, 0].astype(F32) + recv_b[h, 1, 1].astype(F32)
+            accq[rs, 0:256] + recv_b[h, 0, 0].astype(F32) + recv_b[h, 1, 1].astype(F32)
         ).astype(BF16)
         out[rs, 256:512] = (
-            mine[:, 256:512] + recv_b[h, 0, 1].astype(F32) + recv_b[h, 1, 0].astype(F32)
+            accq[rs, 256:512] + recv_b[h, 0, 1].astype(F32) + recv_b[h, 1, 0].astype(F32)
         ).astype(BF16)
 
     block(0, cl, True)
-    block(1, cu, True)
-    lax.fori_loop(1, REACH + 1, lower_step, 0)
-    finish(0)
-    at_copy(0).start()
-    for i in range(4):
-        wo_copy(i).wait()
-        wos_copy(i).wait_recv()
-    lax.fori_loop(1, 3, upper_step, 0)
-    scatter_first(0)
-    lax.fori_loop(3, 7, upper_step, 0)
-    scatter_second(0)
-    lax.fori_loop(7, REACH + 1, upper_step, 0)
+
+    def main_step(i, carry):
+        e = entry(i)
+        p = lax.rem(e, 64)
+
+        @pl.when(lax.rem(lax.div(e, 1024), 2) == 1)
+        def _():
+            kv_copy(p, 0).wait_recv()
+
+        pass_on(e, lambda c: c.start())
+        s = lax.div(p, 2)
+        whole = lax.div(e, 2048) == 1
+
+        @pl.when(whole & (s < d) & (s >= d - REACH))
+        def _():
+            block(0, s, False)
+
+        @pl.when(i == at_whole)
+        def _():
+            finish(0)
+            at_copy(0).start()
+            block(1, cu, True)
+
+        @pl.when(whole & (s >= 22 - d) & (s <= 30 - d))
+        def _():
+            block(1, s, False)
+
+        @pl.when(i == at_first)
+        def _():
+            for k in range(4):
+                wo_copy(k).wait()
+                wos_copy(k).wait_recv()
+            scatter_first(0)
+
+        @pl.when(i == at_second)
+        def _():
+            scatter_second(0)
+            scatter_mine(0)
+
+        return carry
+
+    lax.fori_loop(at_query, n_entries, main_step, 0)
     finish(1)
     at_copy(1).start()
+
+    def drain(i, carry):
+        pass_on(entry(i), lambda c: c.wait_send())
+        return carry
+
+    lax.fori_loop(0, n_entries, drain, 0)
+    scatter_first(1)
     scatter_last(0)
-    scatter_first(1)
     scatter_second(1)
-    scatter_last(1)
-
-    kv_sends(lambda c: c.wait_send())
+    scatter_mine(1)
     for i in range(4):
         wos_copy(i).wait_send()
     for h in range(2):
         at_copy(h).wait_send()
+    scatter_last(1)
+    for h in range(2):
         for way in range(2):
             a_copy(h, way).wait_send()
             for piece in range(2):
@@ -354,7 +429,7 @@
             pltpu.VMEM((rows, 2 * HD), F32),
             pltpu.VMEM((rows, GROUP * HD), F32),
             pltpu.VMEM((rows, HD), F32),
-            pltpu.VMEM((2 * N_CP, 2 * STRETCH, HD), BF16),
+            pltpu.VMEM((4 * N_CP, STRETCH, HD), BF16),
             pltpu.VMEM((2, GROUP * STRETCH, HD), BF16),
             pltpu.VMEM((2, 8, STRETCH), F32),
             pltpu.VMEM((2, GROUP, HD + ONES, STRETCH), F32),
@@ -370,8 +445,8 @@
             dma((4,)),
             dma((4,)),
             dma((4,)),
-            dma((2 * REACH + N_CP - 1,)),
-            dma((2 * N_CP,)),
+            dma((4, 4 * N_CP)),
+            dma((4 * N_CP,)),
             dma((2,)),
             dma((2,)),
             dma((2, 2)),

time: 78.6 us -> 64 us (0.81)
  the two profiles are of different devices: /device:TPU:29 before, /device:TPU:24 now
where the time goes in v2:
time: 64 us; the launch traced here: 63.7 us
  Pallas kernels  59.1 us (92%)
  local copies, waits for them, and re-layouts  4.55 us (7%)
    pallas_call x1, Pallas kernels, step(): pl.pallas_call(kernel, out_shape=jax.ShapeDtypeStruct((rows, 512), BF16),...  59.1 us
    unnamed x1, local copies, waits for them, and re-layouts  1.87 us
    reshape x1, local copies, waits for them, and re-layouts, step(): doc_ids.reshape(2 * N_CP, STRETCH)  1.38 us
    reshape x1, local copies, waits for them, and re-layouts, step(): gain.reshape(1, D)  1.3 us

profile of v2, /device:TPU:24, one launch (start us, length us, event | category | flops | bytes accessed | tf_op | source)
XLA Modules:
  0.0 63.7 jit_solution(113995357952954510)
XLA Ops:
  0.0 1.3 %reshape.6.gain = bf16[1,4096]{1,0:T(2,128)(2,1)} reshape(bf16[4096]{0:T(1024)(128)(2,1)} %param.10) | data formatting | bytes 16384 | tf_op jit(solution)/shard_map/reshape | solution.py:462
  1.3 1.4 %reshape.7.docs = s32[32,256]{1,0:T(8,128)} reshape(s32[8192]{0:T(1024)} %param.15) | data formatting | bytes 65536 | tf_op jit(solution)/shard_map/reshape | solution.py:463
  2.7 59.1 %block.1 = bf16[512,512]{1,0:T(8,128)(2,1)} custom-call(bf16[512,4096]{1,0:T(8,128)(2,1)} %tokens.1, bf16[1,4096]{1,0:T(2,128)(2,1)} %reshape.6.gain, bf16[4096,512]{1,0:T(8,128)(2,1)} %wq.1, bf16[4096,128]{1,0:T(8,128)(2,1)} %wk.1, bf16[4096,128]{1,0:T(8,128)(2,1)} %wv.1, bf16[512,4096]{1,0:T(8,128)(2,1)} %wo.1, s32[32,256]{1,0:T(8,128)} %reshape.7.docs, ...), custom_call_target="tpu_custom_call" | custom-call | tf_op jit(solution)/shard_map/block/pallas_call | solution.py:417
  61.8 1.9 %copy.11 = bf16[512,512]{1,0:T(8,128)(2,1)} copy(bf16[512,512]{1,0:T(8,128)(2,1)} %block.1) | data formatting | bytes 1048576

commit v3 on v2

v3 whole, which is shorter than its diff:
```python
import math

import jax
import jax.numpy as jnp
import numpy as np
from jax import lax
from jax.experimental import pallas as pl
from jax.experimental.pallas import tpu as pltpu
from jax.sharding import PartitionSpec as P

D = 4096
HEADS = 32
HD = 128
GROUP = 4
STRETCH = 256
N_CP = 16
REACH = 9
CHUNK = 512
N_CHUNK = D // CHUNK
NEG = -1e30
EPS = 1e-05
THETA = 500000.0
QSCALE = math.log2(math.e) / math.sqrt(HD)
ONES = 16
F32 = jnp.float32
BF16 = jnp.bfloat16

TABLE = [
    [192, 257, 256, 193, 1271, 1080, 1270, 1081, 452668, 121, 1263, 1072, 468021, 1198, 1137, 500788, 388096, 401588, 437248, 1196, 1074, 181, 1069, 369971, 419898, 486400],
    [258, 67, 189, 66, 259, 188, 1280, 1269, 1082, 1025, 1268, 5179, 187, 1260, 1075, 435255, 486400, 1133, 1202, 1078, 118, 2104, 368826, 418927, 452650, 470016, 1070, 354352, 388096, 404480],
    [68, 261, 186, 260, 69, 187, 1347, 1203, 1081, 1090, 1202, 21560, 420864, 115, 467128, 1280, 1258, 1025, 1131, 6196, 1200, 1073, 1324, 352370, 437248, 1133, 403496, 370742, 338944, 452654, 388096],
    [262, 120, 185, 263, 184, 121, 1152, 1284, 1136, 256, 1153, 1029, 5233, 39936, 401585, 1283, 1192, 1079, 1026, 1193, 21558, 1139, 1071, 336055, 451882, 1198, 386091, 353330, 420864, 370732, 2086, 321588, 437248],
    [200, 265, 567, 264, 201, 566, 1473, 1583, 1073, 1280, 1646, 175, 1072, 6196, 388096, 174, 111, 1026, 1350, 402599, 437248, 1027, 1287, 21670, 103, 259, 1196, 54829, 319590, 1060, 369701, 173, 112, 2052, 2088, 38187, 165, 304170, 338944, 355328, 419890],
    [266, 75, 180, 565, 74, 267, 564, 181, 1474, 1032, 1580, 1075, 1411, 1097, 1581, 21554, 72704, 72, 173, 1024, 1025, 1285, 5284, 368749, 1284, 1707, 1070, 36964, 256, 1125, 1194, 558, 418863, 305186, 352434, 55302, 387110, 289792, 321584, 403496, 338944],
    [76, 269, 691, 268, 77, 690, 1221, 1291, 1578, 1072, 1412, 1098, 1579, 37937, 89088, 261, 75, 170, 560, 1090, 1027, 1286, 21667, 355328, 1159, 1033, 1058, 53347, 1288, 1192, 70697, 401506, 6144, 107, 177, 1316, 2080, 169, 2092, 1061, 288814, 338944, 272422, 371712, 306176, 388096, 322560],
    [271, 688, 113, 270, 112, 689, 1222, 1292, 1576, 1479, 2056, 1037, 54825, 72704, 262, 104, 169, 1153, 1284, 103493, 39936, 1024, 2080, 5295, 68, 261, 2058, 87214, 338944, 2050, 2078, 22439, 272038, 388096, 256034, 2090, 321580, 288804, 355328, 371712, 306176],
    [208, 273, 559, 272, 209, 558, 1481, 1575, 1065, 1068, 1480, 1574, 1064, 70701, 322560, 166, 103, 556, 1089, 1162, 1295, 337445, 371712, 1024, 1035, 1294, 1188, 102, 4649, 87070, 1350, 118949, 2080, 54599, 104460, 2050, 20574, 2076, 304159, 273408, 38916, 2090, 239650, 257024, 355328, 289792],
    [338, 684, 339, 685, 1482, 1040, 1572, 1067, 1419, 80, 1041, 1061, 1066, 86571, 81, 549, 135338, 1218, 304397, 1570, 1091, 2056, 21772, 141, 70691, 1308, 1127, 1157, 103453, 355328, 1156, 2074, 36965, 2062, 1062, 2048, 118947, 6176, 289792, 55302, 2078, 239656, 224256, 322560, 273408, 257024, 338944],
    [276, 85, 554, 171, 84, 277, 170, 555, 1485, 1042, 1571, 1065, 1420, 1107, 1570, 103464, 154624, 1180, 82, 552, 1034, 1099, 87439, 288288, 120206, 335970, 2052, 267, 2064, 1569, 2078, 160, 36963, 138240, 1115, 270505, 2050, 2054, 2056, 168, 21530, 55334, 70685, 2084, 256024, 224256, 322560, 240640, 306176, 207872],
    [278, 552, 233, 279, 232, 553, 1487, 1045, 189985, 1486, 2064, 1044, 120352, 138240, 1566, 276, 96, 161, 1161, 1356, 168973, 1567, 1159, 1032, 103699, 70749, 1030, 1042, 54438, 1116, 153610, 87193, 2052, 1122, 38436, 1048, 1059, 1061, 271399, 256026, 240640, 207872, 289792, 306176, 322560, 224256],
    [88, 153, 551, 152, 89, 550, 1233, 1056, 206373, 1232, 1057, 136740, 273408, 1566, 97, 304201, 1170, 545, 70728, 1043, 153622, 187392, 1103, 189983, 257024, 1102, 120842, 89088, 170004, 175104, 104460, 55302, 239644, 2074, 223266, 289792],
    [91, 548, 165, 90, 164, 549, 538, 155, 1170, 1112, 222754, 1235, 1049, 153123, 203776, 1565, 82, 1162, 156753, 205844, 1163, 1040, 86555, 74, 1173, 136737, 1037, 169503, 286861, 103436, 2056, 163, 1052, 71702, 184482, 173086, 120846, 238624, 191488, 257024, 273408],
    [92, 162, 547, 93, 546, 163, 540, 157, 1172, 1115, 239136, 1173, 1114, 169502, 220160, 1695, 85, 1101, 173080, 222358, 1036, 102939, 185495, 2066, 152090, 201753, 541, 158, 2062, 120848, 536, 135328, 2058, 87073, 257024, 191488, 158720, 207872, 142336, 273408],
    [224, 545, 158, 544, 97, 606, 159, 1238, 1049, 1052, 254495, 1239, 1048, 185885, 203776, 236544, 1041, 1051, 153, 540, 188511, 2062, 1168, 1050, 537, 118876, 1108, 1045, 536, 135329, 220160, 1100, 1037, 168474, 105472, 2066, 151645, 204890, 240640, 125952, 142336, 224256, 175104, 158720],
]
MARKS = [
    [4, 6, 6, 6, 6, 8, 6, 6, 6, 4, 8, 6, 6, 8, 8, 7],
    [4, 11, 19, 20, 35, 35, 32, 31, 40, 39, 42, 34, 31, 36, 33, 36],
    [8, 16, 24, 24, 39, 38, 40, 34, 44, 43, 46, 39, 200, 39, 36, 39],
    [21, 200, 200, 200, 200, 200, 200, 200, 200, 200, 200, 200, 200, 200, 200, 200],
    [26, 30, 31, 33, 41, 41, 47, 41, 46, 47, 50, 46, 36, 41, 40, 44],
]
ENTRIES = max(len(row) for row in TABLE)
SENDS = [sum((e // (64 << k)) % 2 for e in row for k in range(4)) for row in TABLE]


def rope_tables():
    half = HD // 2
    freqs = THETA ** (-2.0 * np.arange(half) / HD)
    inner = np.arange(STRETCH)[:, None] * freqs[None, :]
    outer = (np.arange(2 * N_CP) * STRETCH)[:, None] * freqs[None, :]

    def both(angles):
        c, s = np.cos(angles), np.sin(angles)
        return np.stack([np.concatenate([c, c], 1), np.concatenate([s, s], 1)])

    return both(inner).astype(np.float32), both(outer).astype(np.float32)


def kernel(
    tokens, gain, wq, wk, wv, wo, docs, rope_in, rope_out, out,
    x, xg, wkv, wqv, wo_own, wo_sib, acckv, accq, ssq, kvbuf, qs,
    m_ref, acc_ref, attn_own, attn_sib, send_a, recv_a, send_b, recv_b, qstart,
    gain_in, gain_row, doc_in, r_in, r_out, result,
    in_sems, x_sems, wo_sem, wos_send, wos_recv, kv_send, kv_recv,
    rs_send, at_recv, a_recv, b_recv, out_sems,
):
    d = lax.axis_index("cp")
    t = lax.axis_index("tp")
    z, core = t // 2, t % 2
    sib = t + 1 - 2 * core
    t_up = lax.rem(z + 1, 4) * 2 + core
    t_dn = lax.rem(z + 3, 4) * 2 + core
    zs = [z, lax.rem(z + 1, 4), lax.rem(z + 3, 4), lax.rem(z + 2, 4)]
    cl, cu = d, 2 * N_CP - 1 - d
    px, py = lax.rem(d, 4), lax.div(d, 4)
    beside = [
        py * 4 + lax.rem(px + 1, 4),
        py * 4 + lax.rem(px + 3, 4),
        lax.rem(py + 1, 4) * 4 + px,
        lax.rem(py + 3, 4) * 4 + px,
    ]

    def x_copy(i):
        cols = pl.ds(i * CHUNK, CHUNK)
        return pltpu.make_async_copy(tokens.at[:, cols], x.at[:, cols], x_sems.at[i])

    first_copies = [
        pltpu.make_async_copy(docs, doc_in, in_sems.at[0]),
        pltpu.make_async_copy(gain, gain_in, in_sems.at[1]),
        pltpu.make_async_copy(wk, wkv.at[:, 0:HD], in_sems.at[2]),
        pltpu.make_async_copy(wv, wkv.at[:, HD : 2 * HD], in_sems.at[3]),
    ]
    rope_copies = [
        pltpu.make_async_copy(rope_in, r_in, in_sems.at[4]),
        pltpu.make_async_copy(rope_out, r_out, in_sems.at[5]),
    ]
    wq_copy = pltpu.make_async_copy(wq, wqv, in_sems.at[6])

    def wo_copy(i):
        cols = pl.ds(pl.multiple_of((2 * i + core) * 512, 512), 512)
        return pltpu.make_async_copy(wo.at[:, cols], wo_own.at[i], wo_sem)

    for c in first_copies:
        c.start()
    for i in range(N_CHUNK):
        x_copy(i).start()
    for c in rope_copies:
        c.start()

    barrier = pltpu.get_barrier_semaphore()
    for e in beside:
        pl.semaphore_signal(barrier, 1, device_id={"cp": e, "tp": t})
    for other in (sib, t_up, t_dn):
        pl.semaphore_signal(barrier, 1, device_id={"cp": d, "tp": other})

    here = [(d == e).astype(jnp.int32) for e in range(N_CP)]

    def pick(values):
        total = jnp.int32(0)
        for e, v in enumerate(values):
            if v:
                total = total + here[e] * v
        return total

    words = [pick([row[i] if i < len(row) else 0 for row in TABLE]) for i in range(ENTRIES)]

    def chosen(values, i):
        while len(values) > 1:
            low = lax.rem(i, 2) == 0
            values = [
                jnp.where(low, values[k], values[k + 1]) if k + 1 < len(values) else values[k]
                for k in range(0, len(values), 2)
            ]
            i = lax.div(i, 2)
        return values[0]

    def entry(i):
        return chosen(words, i)

    at_query, at_whole, at_first, at_second, n_entries = [pick(m) for m in MARKS]
    n_sends = pick(SENDS)

    for c in first_copies[:2]:
        c.wait()
    table = doc_in[...].reshape(64, 128)
    rows = [
        doc_in[pl.ds(pl.multiple_of(c * STRETCH, STRETCH), STRETCH)].reshape(1, STRETCH) for c in (cl, cu)
    ]
    for i in range(N_CHUNK):
        cols = slice(i * CHUNK, (i + 1) * CHUNK)
        gain_row[:, cols] = gain_in[cols].astype(F32).reshape(1, CHUNK)
    starts = [jnp.zeros((1, STRETCH), F32) for _ in rows]
    for v in range(1, 16):
        below = jnp.where(table < v, 1.0, 0.0)
        count = jnp.sum(jnp.sum(below, axis=0, keepdims=True), axis=1, keepdims=True)
        starts = [jnp.where(r >= v, count, s) for r, s in zip(rows, starts)]
    qstart[0:1, :] = starts[0].astype(jnp.int32)
    qstart[1:2, :] = starts[1].astype(jnp.int32)
    m_ref[...] = jnp.full_like(m_ref, NEG)
    acc_ref[...] = jnp.zeros_like(acc_ref)

    acckv[...] = jnp.zeros_like(acckv)
    ssq[...] = jnp.zeros_like(ssq)
    for c in first_copies[2:]:
        c.wait()

    def kv_step(i, carry):
        x_copy(i).wait()

        @pl.when(i == N_CHUNK // 2)
        def _():
            wq_copy.start()

        cols = pl.ds(pl.multiple_of(i * CHUNK, CHUNK), CHUNK)
        xf = x[:, cols].astype(F32)
        sq = xf * xf
        ssq[...] += sq[:, 0:128] + sq[:, 128:256] + sq[:, 256:384] + sq[:, 384:512]
        scaled = (xf * gain_row[:, cols]).astype(BF16)
        xg[:, cols] = scaled
        acckv[...] += jnp.dot(scaled, wkv[cols, :], preferred_element_type=F32)
        return carry

    lax.fori_loop(0, N_CHUNK, kv_step, 0)
    for i in range(4):
        wo_copy(i).start()
    for c in rope_copies:
        c.wait()
    mean = jnp.sum(ssq[...], axis=1, keepdims=True) * (1.0 / D)
    factor = lax.rsqrt(mean + EPS)
    ssq[...] = jnp.broadcast_to(factor, (2 * STRETCH, HD))

    sign = jnp.where(lax.broadcasted_iota(jnp.int32, (1, HD), 1) < HD // 2, -1.0, 1.0)

    def rope(h):
        c = cl if h == 0 else cu
        co, so = r_out[0, pl.ds(c, 1), :], r_out[1, pl.ds(c, 1), :]
        ci, si = r_in[0], r_in[1]
        return ci * co - si * so, (ci * so + si * co) * sign

    for h, c in ((0, cl), (1, cu)):
        rs = slice(h * STRETCH, (h + 1) * STRETCH)
        cosine, sine = rope(h)
        kf = acckv[rs, 0:HD] * ssq[rs, :]
        kvbuf[2 * c] = (kf * cosine + pltpu.roll(kf, HD // 2, 1) * sine).astype(BF16)
        vf = acckv[rs, HD : 2 * HD] * ssq[rs, :]
        kvbuf[2 * c + 1, 0:HD, :] = vf[0:HD, :].T.astype(BF16)
        kvbuf[2 * c + 1, HD : 2 * HD, :] = vf[HD : 2 * HD, :].T.astype(BF16)

    pl.semaphore_wait(barrier, 7)

    def kv_slot(p, e):
        s = lax.div(p, 2)
        lower = (s < e) & (s >= e - REACH)
        return lax.rem(s, REACH) * 2 + lax.rem(p, 2) + jnp.where(lower, 0, 2 * REACH)

    def kv_copy(p, way):
        return pltpu.make_async_remote_copy(
            src_ref=kvbuf.at[p], dst_ref=kvbuf.at[p], send_sem=kv_send,
            recv_sem=kv_recv.at[kv_slot(p, beside[way])], device_id={"cp": beside[way], "tp": t},
        )

    def kv_wait(p):
        pltpu.make_async_remote_copy(
            src_ref=kvbuf.at[p], dst_ref=kvbuf.at[p], send_sem=kv_send,
            recv_sem=kv_recv.at[kv_slot(p, d)], device_id={"cp": beside[0], "tp": t},
        ).wait_recv()

    def pass_on(e, act):
        p, ways = lax.rem(e, 64), lax.rem(lax.div(e, 64), 16)

        @pl.when(ways > 0)
        def _():
            for way in range(4):
                @pl.when(lax.rem(lax.div(ways, 2**way), 2) == 1)
                def _():
                    act(kv_copy(p, way))

    def send_only(i, carry):
        pass_on(entry(i), lambda c: c.start())
        return carry

    lax.fori_loop(0, at_query, send_only, 0)

    def wos_copy(i):
        cols = pl.ds(pl.multiple_of((2 * i + 1 - core) * 512, 512), 512)
        return pltpu.make_async_remote_copy(
            src_ref=wo.at[:, cols], dst_ref=wo_sib.at[i], send_sem=wos_send,
            recv_sem=wos_recv, device_id={"cp": d, "tp": sib},
        )

    for i in range(4):
        wos_copy(i).start()

    wq_copy.wait()

    def q_step(i, carry):
        cols = pl.ds(pl.multiple_of(i * 256, 256), 256)
        accq[:, cols] = jnp.dot(xg[...], wqv[:, cols], preferred_element_type=F32)
        return carry

    lax.fori_loop(0, 2, q_step, 0)
    for h in range(2):
        rs = slice(h * STRETCH, (h + 1) * STRETCH)
        cosine, sine = rope(h)
        scale = ssq[rs, :] * QSCALE
        for g in range(GROUP):
            qf = accq[rs, g * HD : (g + 1) * HD] * scale
            qs[h, g * STRETCH : (g + 1) * STRETCH, :] = (
                qf * cosine + pltpu.roll(qf, HD // 2, 1) * sine
            ).astype(BF16)

    key_row = lax.broadcasted_iota(jnp.int32, (STRETCH, STRETCH), 0)
    query_col = lax.broadcasted_iota(jnp.int32, (STRETCH, STRETCH), 1)
    ones = jnp.ones((ONES, STRETCH), BF16)

    def block(h, s, own):
        keys = kvbuf[2 * s]
        vt = jnp.concatenate([kvbuf[2 * s + 1, 0:HD, :], kvbuf[2 * s + 1, HD : 2 * HD, :]], axis=1)
        vt = jnp.concatenate([vt, ones], axis=0)
        mask = key_row >= qstart[h : h + 1, :] - s * STRETCH
        if own:
            mask = mask & (key_row <= query_col)
        scores = [
            lax.dot_general(
                keys, qs[h, g * STRETCH : (g + 1) * STRETCH, :], (((1,), (1,)), ((), ())),
                preferred_element_type=F32,
            )
            for g in range(GROUP)
        ]
        before = [m_ref[h, g : g + 1, :] for g in range(GROUP)]
        held = [acc_ref[h, g] for g in range(GROUP)]
        tops, added = [], []
        for g in range(GROUP):
            sc = jnp.where(mask, scores[g], NEG)
            top = jnp.maximum(jnp.max(sc, axis=0, keepdims=True), before[g])
            weights = jnp.exp2(sc - top).astype(BF16)
            tops.append(top)
            added.append(jnp.dot(vt, weights, preferred_element_type=F32))
        for g in range(GROUP):
            acc_ref[h, g] = held[g] * jnp.exp2(before[g] - tops[g]) + added[g]
            m_ref[h, g : g + 1, :] = tops[g]

    def finish(h):
        for g in range(GROUP):
            o = acc_ref[h, g, 0:HD, :] / acc_ref[h, g, HD : HD + 1, :]
            attn_own[h, :, g * HD : (g + 1) * HD] = o.T.astype(BF16)

    def at_copy(h):
        return pltpu.make_async_remote_copy(
            src_ref=attn_own.at[h], dst_ref=attn_sib.at[h], send_sem=rs_send,
            recv_sem=at_recv.at[h], device_id={"cp": d, "tp": sib},
        )

    def project(h, i):
        zz = zs[i]
        return jnp.dot(attn_own[h], wo_own[zz], preferred_element_type=F32) + jnp.dot(
            attn_sib[h], wo_sib[zz], preferred_element_type=F32
        )

    def a_copy(h, way):
        return pltpu.make_async_remote_copy(
            src_ref=send_a.at[h, way], dst_ref=recv_a.at[h, way], send_sem=rs_send,
            recv_sem=a_recv.at[h, way], device_id={"cp": d, "tp": t_up if way == 0 else t_dn},
        )

    def b_copy(h, way, piece):
        return pltpu.make_async_remote_copy(
            src_ref=send_b.at[h, way, piece], dst_ref=recv_b.at[h, way, piece],
            send_sem=rs_send, recv_sem=b_recv.at[h],
            device_id={"cp": d, "tp": t_up if way == 0 else t_dn},
        )

    summed = [slice(0, 256), slice(256, 512)]
    plain = [slice(256, 512), slice(0, 256)]

    def scatter_first(h):
        at_copy(h).wait_recv()
        far = project(h, 3)
        for way in range(2):
            send_a[h, way] = far[:, summed[way]].astype(BF16)
            a_copy(h, way).start()
        for way in range(2):
            near = project(h, 1 + way)
            accq[h * STRETCH : (h + 1) * STRETCH, way * 256 : (way + 1) * 256] = near[:, summed[way]]
            send_b[h, way, 1] = near[:, plain[way]].astype(BF16)
            b_copy(h, way, 1).start()

    def scatter_second(h):
        for way in range(2):
            a_copy(h, way).wait_recv()
            own = accq[h * STRETCH : (h + 1) * STRETCH, way * 256 : (way + 1) * 256]
            send_b[h, way, 0] = (own + recv_a[h, way].astype(F32)).astype(BF16)
            b_copy(h, way, 0).start()

    def scatter_mine(h):
        accq[h * STRETCH : (h + 1) * STRETCH, :] = project(h, 0)

    def scatter_last(h):
        rs = slice(h * STRETCH, (h + 1) * STRETCH)
        pltpu.make_async_copy(recv_b.at[h], recv_b.at[h], b_recv.at[h]).wait()
        result[rs, 0:256] = (
            accq[rs, 0:256] + recv_b[h, 0, 0].astype(F32) + recv_b[h, 1, 1].astype(F32)
        ).astype(BF16)
        result[rs, 256:512] = (
            accq[rs, 256:512] + recv_b[h, 0, 1].astype(F32) + recv_b[h, 1, 0].astype(F32)
        ).astype(BF16)
        out_copy(h).start()

    def out_copy(h):
        rs = slice(h * STRETCH, (h + 1) * STRETCH)
        return pltpu.make_async_copy(result.at[rs], out.at[rs], out_sems.at[h])

    block(0, cl, True)

    @pl.when(at_whole < at_query)
    def _():
        finish(0)
        at_copy(0).start()
        block(1, cu, True)

    def weights_here():
        pltpu.make_async_copy(wo_own, wo_own, wo_sem).wait()
        pltpu.make_async_copy(wo_sib, wo_sib, wos_recv).wait()

    def main_step(i, carry):
        e = entry(i)
        p = lax.rem(e, 64)
        kind = lax.rem(lax.div(e, 1024), 4)
        job = lax.rem(lax.div(e, 4096), 4)
        s = lax.div(e, 16384)

        @pl.when(kind == 1)
        def _():
            kv_wait(p)

        @pl.when(kind == 2)
        def _():
            kv_wait(p)
            kv_wait(p + 1)

        pass_on(e, lambda c: c.start())

        @pl.when(job == 1)
        def _():
            block(0, s, False)

        @pl.when(i == at_whole)
        def _():
            finish(0)
            at_copy(0).start()
            block(1, cu, True)

        @pl.when(job == 2)
        def _():
            block(1, s, False)

        @pl.when(i == at_first)
        def _():
            weights_here()
            scatter_first(0)

        @pl.when(i == at_second)
        def _():
            scatter_second(0)
            scatter_mine(0)

        return carry

    lax.fori_loop(at_query, n_entries, main_step, 0)
    finish(1)
    at_copy(1).start()

    @pl.when(at_first >= n_entries)
    def _():
        weights_here()
        scatter_first(0)

    scatter_first(1)

    @pl.when(at_second >= n_entries)
    def _():
        scatter_second(0)
        scatter_mine(0)

    scatter_second(1)
    scatter_mine(1)
    scatter_last(0)
    scatter_last(1)
    for count in sorted(set(SENDS)):
        @pl.when(n_sends == count)
        def _():
            pltpu.make_async_copy(kvbuf.at[0:count], kvbuf.at[0:count], kv_send).wait()
    pltpu.make_async_copy(wo_sib, wo_sib, wos_send).wait()
    pltpu.make_async_copy(wo_own, wo_own, rs_send).wait()
    for h in range(2):
        out_copy(h).wait()


def step(tokens, gain, w_query, w_key, w_value, w_out, doc_ids):
    rope_in, rope_out = rope_tables()
    any_space = pl.BlockSpec(memory_space=pl.ANY)
    rows = 2 * STRETCH
    dma = pltpu.SemaphoreType.DMA
    return pl.pallas_call(
        kernel,
        out_shape=jax.ShapeDtypeStruct((rows, 512), BF16),
        in_specs=[any_space] * 9,
        out_specs=any_space,
        scratch_shapes=[
            pltpu.VMEM((rows, D), BF16),
            pltpu.VMEM((rows, D), BF16),
            pltpu.VMEM((D, 2 * HD), BF16),
            pltpu.VMEM((D, GROUP * HD), BF16),
            pltpu.VMEM((4, 512, 512), BF16),
            pltpu.VMEM((4, 512, 512), BF16),
            pltpu.VMEM((rows, 2 * HD), F32),
            pltpu.VMEM((rows, GROUP * HD), F32),
            pltpu.VMEM((rows, HD), F32),
            pltpu.VMEM((4 * N_CP, STRETCH, HD), BF16),
            pltpu.VMEM((2, GROUP * STRETCH, HD), BF16),
            pltpu.VMEM((2, 8, STRETCH), F32),
            pltpu.VMEM((2, GROUP, HD + ONES, STRETCH), F32),
            pltpu.VMEM((2, STRETCH, 512), BF16),
            pltpu.VMEM((2, STRETCH, 512), BF16),
            pltpu.VMEM((2, 2, STRETCH, 256), BF16),
            pltpu.VMEM((2, 2, STRETCH, 256), BF16),
            pltpu.VMEM((2, 2, 2, STRETCH, 256), BF16),
            pltpu.VMEM((2, 2, 2, STRETCH, 256), BF16),
            pltpu.VMEM((8, STRETCH), jnp.int32),
            pltpu.VMEM((D,), BF16),
            pltpu.VMEM((1, D), F32),
            pltpu.VMEM((2 * N_CP * STRETCH,), jnp.int32),
            pltpu.VMEM((2, STRETCH, HD), F32),
            pltpu.VMEM((2, 2 * N_CP, HD), F32),
            pltpu.VMEM((rows, 512), BF16),
            dma((7,)),
            dma((N_CHUNK,)),
            dma,
            dma,
            dma,
            dma,
            dma((4 * REACH,)),
            dma,
            dma((2,)),
            dma((2, 2)),
            dma((2,)),
            dma((2,)),
        ],
        compiler_params=pltpu.CompilerParams(
            collective_id=0, has_side_effects=True, vmem_limit_bytes=60 * 1024 * 1024
        ),
        name="block",
    )(
        tokens, gain, w_query, w_key, w_value, w_out,
        doc_ids, jnp.asarray(rope_in), jnp.asarray(rope_out),
    )


def solution(mesh):
    in_specs = (P("cp", None), P(), P(None, "tp"), P(None, "tp"), P(None, "tp"), P("tp", None), P())
    return jax.shard_map(step, mesh=mesh, in_specs=in_specs, out_specs=P("cp", "tp"), check_vma=False)
```

time: 64 us -> 53.1 us (0.83)
  Pallas kernels: 59.1 us -> 51 us
  local copies, waits for them, and re-layouts: 4.55 us -> 1.87 us
    pallas_call x1, Pallas kernels: 59.1 us -> 51 us  [step(): pl.pallas_call(kernel, out_shape=jax.ShapeDtypeStruct((rows, 512), BF16),...]
    reshape x2 -> x0, local copies, waits for them, and re-layouts: 2.68 us -> none  [the longest x1 1.38 us: step(): doc_ids.reshape(2 * N_CP, STRETCH)]
where the time goes in v3:
time: 53.1 us; the launch traced here: 52.9 us
  Pallas kernels  51 us (96%)
  local copies, waits for them, and re-layouts  1.87 us (4%)
    pallas_call x1, Pallas kernels, step(): pl.pallas_call(kernel, out_shape=jax.ShapeDtypeStruct((rows, 512), BF16),...  51 us
    unnamed x1, local copies, waits for them, and re-layouts  1.87 us

profile of v3, /device:TPU:24, one launch (start us, length us, event | category | flops | bytes accessed | tf_op | source)
XLA Modules:
  0.0 52.9 jit_solution(1481660319612976049)
XLA Ops:
  0.0 51.0 %block.1 = bf16[512,512]{1,0:T(8,128)(2,1)} custom-call(bf16[512,4096]{1,0:T(8,128)(2,1)} %tokens.1, bf16[4096]{0:T(1024)(128)(2,1)} %gain.1, bf16[4096,512]{1,0:T(8,128)(2,1)} %wq.1, bf16[4096,128]{1,0:T(8,128)(2,1)} %wk.1, bf16[4096,128]{1,0:T(8,128)(2,1)} %wv.1, bf16[512,4096]{1,0:T(8,128)(2,1)} %wo.1, s32[8192]{0:T(1024)} %docs.1, ...), custom_call_target="tpu_custom_call" | custom-call | tf_op jit(solution)/shard_map/block/pallas_call | solution.py:475
  51.1 1.9 %copy.11 = bf16[512,512]{1,0:T(8,128)(2,1)} copy(bf16[512,512]{1,0:T(8,128)(2,1)} %block.1) | data formatting | bytes 1048576

commit v4 on v3

--- a/solution.py
+++ b/solution.py
@@ -26,29 +26,29 @@
 BF16 = jnp.bfloat16
 
 TABLE = [
-    [192, 257, 256, 193, 1271, 1080, 1270, 1081, 452668, 121, 1263, 1072, 468021, 1198, 1137, 500788, 388096, 401588, 437248, 1196, 1074, 181, 1069, 369971, 419898, 486400],
-    [258, 67, 189, 66, 259, 188, 1280, 1269, 1082, 1025, 1268, 5179, 187, 1260, 1075, 435255, 486400, 1133, 1202, 1078, 118, 2104, 368826, 418927, 452650, 470016, 1070, 354352, 388096, 404480],
-    [68, 261, 186, 260, 69, 187, 1347, 1203, 1081, 1090, 1202, 21560, 420864, 115, 467128, 1280, 1258, 1025, 1131, 6196, 1200, 1073, 1324, 352370, 437248, 1133, 403496, 370742, 338944, 452654, 388096],
-    [262, 120, 185, 263, 184, 121, 1152, 1284, 1136, 256, 1153, 1029, 5233, 39936, 401585, 1283, 1192, 1079, 1026, 1193, 21558, 1139, 1071, 336055, 451882, 1198, 386091, 353330, 420864, 370732, 2086, 321588, 437248],
-    [200, 265, 567, 264, 201, 566, 1473, 1583, 1073, 1280, 1646, 175, 1072, 6196, 388096, 174, 111, 1026, 1350, 402599, 437248, 1027, 1287, 21670, 103, 259, 1196, 54829, 319590, 1060, 369701, 173, 112, 2052, 2088, 38187, 165, 304170, 338944, 355328, 419890],
-    [266, 75, 180, 565, 74, 267, 564, 181, 1474, 1032, 1580, 1075, 1411, 1097, 1581, 21554, 72704, 72, 173, 1024, 1025, 1285, 5284, 368749, 1284, 1707, 1070, 36964, 256, 1125, 1194, 558, 418863, 305186, 352434, 55302, 387110, 289792, 321584, 403496, 338944],
-    [76, 269, 691, 268, 77, 690, 1221, 1291, 1578, 1072, 1412, 1098, 1579, 37937, 89088, 261, 75, 170, 560, 1090, 1027, 1286, 21667, 355328, 1159, 1033, 1058, 53347, 1288, 1192, 70697, 401506, 6144, 107, 177, 1316, 2080, 169, 2092, 1061, 288814, 338944, 272422, 371712, 306176, 388096, 322560],
-    [271, 688, 113, 270, 112, 689, 1222, 1292, 1576, 1479, 2056, 1037, 54825, 72704, 262, 104, 169, 1153, 1284, 103493, 39936, 1024, 2080, 5295, 68, 261, 2058, 87214, 338944, 2050, 2078, 22439, 272038, 388096, 256034, 2090, 321580, 288804, 355328, 371712, 306176],
-    [208, 273, 559, 272, 209, 558, 1481, 1575, 1065, 1068, 1480, 1574, 1064, 70701, 322560, 166, 103, 556, 1089, 1162, 1295, 337445, 371712, 1024, 1035, 1294, 1188, 102, 4649, 87070, 1350, 118949, 2080, 54599, 104460, 2050, 20574, 2076, 304159, 273408, 38916, 2090, 239650, 257024, 355328, 289792],
-    [338, 684, 339, 685, 1482, 1040, 1572, 1067, 1419, 80, 1041, 1061, 1066, 86571, 81, 549, 135338, 1218, 304397, 1570, 1091, 2056, 21772, 141, 70691, 1308, 1127, 1157, 103453, 355328, 1156, 2074, 36965, 2062, 1062, 2048, 118947, 6176, 289792, 55302, 2078, 239656, 224256, 322560, 273408, 257024, 338944],
-    [276, 85, 554, 171, 84, 277, 170, 555, 1485, 1042, 1571, 1065, 1420, 1107, 1570, 103464, 154624, 1180, 82, 552, 1034, 1099, 87439, 288288, 120206, 335970, 2052, 267, 2064, 1569, 2078, 160, 36963, 138240, 1115, 270505, 2050, 2054, 2056, 168, 21530, 55334, 70685, 2084, 256024, 224256, 322560, 240640, 306176, 207872],
-    [278, 552, 233, 279, 232, 553, 1487, 1045, 189985, 1486, 2064, 1044, 120352, 138240, 1566, 276, 96, 161, 1161, 1356, 168973, 1567, 1159, 1032, 103699, 70749, 1030, 1042, 54438, 1116, 153610, 87193, 2052, 1122, 38436, 1048, 1059, 1061, 271399, 256026, 240640, 207872, 289792, 306176, 322560, 224256],
-    [88, 153, 551, 152, 89, 550, 1233, 1056, 206373, 1232, 1057, 136740, 273408, 1566, 97, 304201, 1170, 545, 70728, 1043, 153622, 187392, 1103, 189983, 257024, 1102, 120842, 89088, 170004, 175104, 104460, 55302, 239644, 2074, 223266, 289792],
-    [91, 548, 165, 90, 164, 549, 538, 155, 1170, 1112, 222754, 1235, 1049, 153123, 203776, 1565, 82, 1162, 156753, 205844, 1163, 1040, 86555, 74, 1173, 136737, 1037, 169503, 286861, 103436, 2056, 163, 1052, 71702, 184482, 173086, 120846, 238624, 191488, 257024, 273408],
-    [92, 162, 547, 93, 546, 163, 540, 157, 1172, 1115, 239136, 1173, 1114, 169502, 220160, 1695, 85, 1101, 173080, 222358, 1036, 102939, 185495, 2066, 152090, 201753, 541, 158, 2062, 120848, 536, 135328, 2058, 87073, 257024, 191488, 158720, 207872, 142336, 273408],
-    [224, 545, 158, 544, 97, 606, 159, 1238, 1049, 1052, 254495, 1239, 1048, 185885, 203776, 236544, 1041, 1051, 153, 540, 188511, 2062, 1168, 1050, 537, 118876, 1108, 1045, 536, 135329, 220160, 1100, 1037, 168474, 105472, 2066, 151645, 204890, 240640, 125952, 142336, 224256, 175104, 158720],
+    [256, 193, 192, 257, 1271, 16258104, 1270, 1081, 14673980, 16198656, 121, 1198, 1136, 1077, 1199, 1073, 1076, 12968046, 180, 1069, 11969708, 1075, 1330, 15624250],
+    [66, 259, 189, 258, 67, 188, 1345, 1205, 1082, 1088, 1204, 21563, 117, 14131386, 1260, 1074, 1133, 1203, 2102, 12019768, 116, 187, 14575658, 11478127, 1070, 12970032],
+    [260, 69, 186, 68, 261, 187, 1346, 1202, 1081, 1091, 1203, 562232, 13593600, 114, 184, 1281, 1259, 1072, 1024, 1066, 15209649, 115, 11478069, 106, 1324, 2088, 117, 10888237, 2102, 14525492, 12494894],
+    [262, 120, 185, 263, 184, 121, 1025, 1285, 1264, 1024, 257, 1028, 54513, 13052928, 1282, 1192, 1079, 1027, 1065, 562358, 1138, 14491831, 1198, 1323, 1071, 13493299, 1066, 11888684, 2100, 10397734],
+    [328, 137, 567, 136, 329, 566, 1472, 1582, 1073, 1281, 174, 1647, 1072, 71732, 110, 12509359, 1027, 1286, 1709, 14033009, 1026, 1287, 1594599, 258, 1190, 11854892, 112, 1028, 1285, 14193701, 172, 1188, 2088, 10789930, 1323, 13461554],
+    [266, 75, 693, 74, 267, 692, 1475, 1032, 1580, 1074, 1410, 1097, 1581, 611379, 72, 11968684, 1088, 1025, 1412, 71210, 1285, 1125, 1583, 170, 1124, 1195, 9856046, 12413952, 179, 2054, 2082, 1611111, 1062, 10250288, 2088, 10890240],
+    [268, 77, 690, 76, 269, 691, 1220, 1291, 1579, 260, 1157, 1098, 1578, 1153072, 261, 75, 11428011, 1026, 1091, 1414, 611362, 1159, 1577, 258, 98, 2056, 1123, 2151464, 169, 13113344, 168, 106, 9316384, 8727552, 2084, 2094, 12363820, 10332198],
+    [270, 688, 113, 271, 112, 689, 1222, 1293, 1576, 1479, 2056, 1036, 1693225, 262, 168, 3215465, 1028, 1349, 10888353, 2048, 38062, 260, 104, 2058, 1056, 12330159, 2050, 2078, 612013, 1575, 2082, 1702, 2090, 9167916, 11332608, 9807908],
+    [272, 209, 558, 208, 273, 559, 1480, 1063, 1581, 1481, 1062, 551, 2088, 2233388, 614, 10346663, 1088, 1294, 1573, 11870374, 1089, 2058, 1295, 1572, 2625701, 1055, 1350, 164, 2060, 3266592, 8693063, 1054, 2050, 577631, 12097540, 7596060, 2082, 11298858],
+    [338, 556, 173, 339, 172, 557, 1482, 1041, 1060, 1578, 1419, 1040, 81, 1573, 2774059, 80, 548, 9805994, 1091, 1032, 1420, 1571, 1026, 1097, 660749, 131, 1570, 1309, 3216934, 1156, 1052, 9265252, 1029, 2074, 163, 101, 2048, 38926, 7053474, 2054, 1693728, 1063, 2078, 10233896, 10742784],
+    [276, 85, 170, 555, 84, 277, 554, 171, 1484, 1042, 1570, 1064, 1421, 1107, 1059, 3315241, 1181, 82, 9265699, 1098, 1035, 1422, 2774044, 7677327, 75, 1568, 2052, 267, 2064, 1057, 99, 1167528, 161, 98, 2050, 2054, 661512, 2150569, 7088154, 2084, 2086, 10266648, 8071198],
+    [279, 680, 105, 278, 104, 681, 1486, 1045, 6104609, 1487, 2064, 1044, 3855903, 1568, 276, 95, 5378209, 1160, 1036, 1357, 8136222, 1159, 1033, 2200669, 1030, 2066, 4773031, 1190, 2052, 2058, 2659877, 159, 1052, 7660580, 2072, 2082, 6596634, 7105536],
+    [88, 153, 551, 152, 89, 550, 1232, 1056, 6612517, 1233, 1057, 4396580, 9710592, 1054, 96, 545, 1096, 1170, 544, 1097, 1171, 2070, 4788766, 1102, 8053791, 1103, 2058, 3855900, 95, 5330964, 2060, 1677318, 7513117, 2074, 9136162],
+    [91, 548, 165, 90, 164, 549, 154, 539, 1234, 1048, 7120419, 1235, 1049, 4937250, 6450176, 1564, 88, 1226, 1040, 1044, 1163, 1105, 2822682, 1173, 5379616, 1036, 5531166, 140, 1037, 2056, 2199714, 1053, 8627233, 163, 2070, 3856398, 8053791],
+    [93, 546, 163, 92, 162, 547, 156, 541, 1172, 1115, 7627806, 540, 1173, 1114, 5477920, 6990848, 1057, 85, 1100, 538, 158, 1175, 1037, 2066, 3363358, 1561, 1048, 6443169, 4990102, 539, 3856398, 2064, 536, 2058, 2757663, 5975040, 8006656],
+    [158, 96, 545, 543, 160, 97, 94, 544, 161, 1239, 1049, 8135709, 542, 1110, 1048, 6018076, 153, 7541277, 1040, 1563, 150, 6479967, 2062, 1041, 1050, 144, 536, 4313180, 1108, 1045, 540, 5460127, 1036, 1101, 3908121, 2066, 538, 4821085, 6955099, 4893696],
 ]
 MARKS = [
-    [4, 6, 6, 6, 6, 8, 6, 6, 6, 4, 8, 6, 6, 8, 8, 7],
-    [4, 11, 19, 20, 35, 35, 32, 31, 40, 39, 42, 34, 31, 36, 33, 36],
-    [8, 16, 24, 24, 39, 38, 40, 34, 44, 43, 46, 39, 200, 39, 36, 39],
-    [21, 200, 200, 200, 200, 200, 200, 200, 200, 200, 200, 200, 200, 200, 200, 200],
-    [26, 30, 31, 33, 41, 41, 47, 41, 46, 47, 50, 46, 36, 41, 40, 44],
+    [4, 6, 6, 6, 6, 6, 6, 6, 6, 6, 8, 6, 6, 8, 8, 9],
+    [5, 11, 20, 19, 29, 31, 29, 28, 34, 40, 37, 30, 31, 35, 34, 37],
+    [9, 15, 24, 23, 34, 34, 33, 31, 36, 200, 41, 35, 200, 200, 200, 200],
+    [22, 200, 200, 200, 200, 200, 200, 200, 200, 200, 200, 200, 200, 200, 200, 200],
+    [24, 26, 31, 30, 36, 36, 38, 36, 38, 45, 43, 38, 35, 37, 37, 40],
 ]
 ENTRIES = max(len(row) for row in TABLE)
 SENDS = [sum((e // (64 << k)) % 2 for e in row for k in range(4)) for row in TABLE]
@@ -71,9 +71,9 @@
     tokens, gain, wq, wk, wv, wo, docs, rope_in, rope_out, out,
     x, xg, wkv, wqv, wo_own, wo_sib, acckv, accq, ssq, kvbuf, qs,
     m_ref, acc_ref, attn_own, attn_sib, send_a, recv_a, send_b, recv_b, qstart,
-    gain_in, gain_row, doc_in, r_in, r_out, result,
+    gain_in, gain_row, doc_in, r_in, r_out,
     in_sems, x_sems, wo_sem, wos_send, wos_recv, kv_send, kv_recv,
-    rs_send, at_recv, a_recv, b_recv, out_sems,
+    rs_send, at_recv, a_recv, b_recv,
 ):
     d = lax.axis_index("cp")
     t = lax.axis_index("tp")
@@ -282,15 +282,21 @@
 
     key_row = lax.broadcasted_iota(jnp.int32, (STRETCH, STRETCH), 0)
     query_col = lax.broadcasted_iota(jnp.int32, (STRETCH, STRETCH), 1)
-    ones = jnp.ones((ONES, STRETCH), BF16)
-
-    def block(h, s, own):
-        keys = kvbuf[2 * s]
-        vt = jnp.concatenate([kvbuf[2 * s + 1, 0:HD, :], kvbuf[2 * s + 1, HD : 2 * HD, :]], axis=1)
+    ones = jnp.ones((ONES, 2 * STRETCH), BF16)
+
+    def attend(h, s1, s2):
+        c = jnp.where(h == 0, cl, cu)
+        keys = jnp.concatenate([kvbuf[2 * s1], kvbuf[2 * s2]], axis=0)
+        vt = jnp.concatenate([kvbuf[2 * s + 1, r : r + HD, :] for s in (s1, s2) for r in (0, HD)], axis=1)
         vt = jnp.concatenate([vt, ones], axis=0)
-        mask = key_row >= qstart[h : h + 1, :] - s * STRETCH
-        if own:
-            mask = mask & (key_row <= query_col)
+        begin = qstart[pl.ds(h, 1), :]
+        mask = jnp.concatenate(
+            [
+                (key_row >= begin - s * STRETCH) & (key_row <= query_col + (c - s) * STRETCH)
+                for s in (s1, s2)
+            ],
+            axis=0,
+        )
         scores = [
             lax.dot_general(
                 keys, qs[h, g * STRETCH : (g + 1) * STRETCH, :], (((1,), (1,)), ((), ())),
@@ -369,25 +375,12 @@
     def scatter_last(h):
         rs = slice(h * STRETCH, (h + 1) * STRETCH)
         pltpu.make_async_copy(recv_b.at[h], recv_b.at[h], b_recv.at[h]).wait()
-        result[rs, 0:256] = (
+        out[rs, 0:256] = (
             accq[rs, 0:256] + recv_b[h, 0, 0].astype(F32) + recv_b[h, 1, 1].astype(F32)
         ).astype(BF16)
-        result[rs, 256:512] = (
+        out[rs, 256:512] = (
             accq[rs, 256:512] + recv_b[h, 0, 1].astype(F32) + recv_b[h, 1, 0].astype(F32)
         ).astype(BF16)
-        out_copy(h).start()
-
-    def out_copy(h):
-        rs = slice(h * STRETCH, (h + 1) * STRETCH)
-        return pltpu.make_async_copy(result.at[rs], out.at[rs], out_sems.at[h])
-
-    block(0, cl, True)
-
-    @pl.when(at_whole < at_query)
-    def _():
-        finish(0)
-        at_copy(0).start()
-        block(1, cu, True)
 
     def weights_here():
         pltpu.make_async_copy(wo_own, wo_own, wo_sem).wait()
@@ -398,7 +391,7 @@
         p = lax.rem(e, 64)
         kind = lax.rem(lax.div(e, 1024), 4)
         job = lax.rem(lax.div(e, 4096), 4)
-        s = lax.div(e, 16384)
+        s1, s2 = lax.rem(lax.div(e, 16384), 32), lax.div(e, 524288)
 
         @pl.when(kind == 1)
         def _():
@@ -411,19 +404,14 @@
 
         pass_on(e, lambda c: c.start())
 
-        @pl.when(job == 1)
-        def _():
-            block(0, s, False)
+        @pl.when(job > 0)
+        def _():
+            attend(job - 1, s1, s2)
 
         @pl.when(i == at_whole)
         def _():
             finish(0)
             at_copy(0).start()
-            block(1, cu, True)
-
-        @pl.when(job == 2)
-        def _():
-            block(1, s, False)
 
         @pl.when(i == at_first)
         def _():
@@ -463,8 +451,6 @@
             pltpu.make_async_copy(kvbuf.at[0:count], kvbuf.at[0:count], kv_send).wait()
     pltpu.make_async_copy(wo_sib, wo_sib, wos_send).wait()
     pltpu.make_async_copy(wo_own, wo_own, rs_send).wait()
-    for h in range(2):
-        out_copy(h).wait()
 
 
 def step(tokens, gain, w_query, w_key, w_value, w_out, doc_ids):
@@ -474,9 +460,9 @@
     dma = pltpu.SemaphoreType.DMA
     return pl.pallas_call(
         kernel,
-        out_shape=jax.ShapeDtypeStruct((rows, 512), BF16),
+        out_shape=pltpu.VMEM((rows, 512), BF16),
         in_specs=[any_space] * 9,
-        out_specs=any_space,
+        out_specs=pl.BlockSpec(memory_space=pltpu.VMEM),
         scratch_shapes=[
             pltpu.VMEM((rows, D), BF16),
             pltpu.VMEM((rows, D), BF16),
@@ -503,7 +489,6 @@
             pltpu.VMEM((2 * N_CP * STRETCH,), jnp.int32),
             pltpu.VMEM((2, STRETCH, HD), F32),
             pltpu.VMEM((2, 2 * N_CP, HD), F32),
-            pltpu.VMEM((rows, 512), BF16),
             dma((7,)),
             dma((N_CHUNK,)),
             dma,
@@ -515,7 +500,6 @@
             dma((2,)),
             dma((2, 2)),
             dma((2,)),
-            dma((2,)),
         ],
         compiler_params=pltpu.CompilerParams(
             collective_id=0, has_side_effects=True, vmem_limit_bytes=60 * 1024 * 1024

time: 53.1 us -> 51.3 us (0.966)
  local copies, waits for them, and re-layouts: 1.87 us -> 0.8 us
  Pallas kernels: 51 us -> 50.4 us
    unnamed x1, local copies, waits for them, and re-layouts: 1.87 us -> 0.8 us
    pallas_call x1, Pallas kernels: 51 us -> 50.4 us  [step(): pl.pallas_call(kernel, out_shape=pltpu.VMEM((rows, 512), BF16), in_specs=...]
where the time goes in v4:
time: 51.3 us; the launch traced here: 51.2 us
  Pallas kernels  50.4 us (98%)
  local copies, waits for them, and re-layouts  0.8 us (2%)
    pallas_call x1, Pallas kernels, step(): pl.pallas_call(kernel, out_shape=pltpu.VMEM((rows, 512), BF16), in_specs=...  50.4 us

profile of v4, /device:TPU:24, one launch (start us, length us, event | category | flops | bytes accessed | tf_op | source)
XLA Modules:
  0.0 51.2 jit_solution(12577592970681823106)
XLA Ops:
  0.0 50.4 %block.1 = bf16[512,512]{1,0:T(8,128)(2,1)S(1)} custom-call(bf16[512,4096]{1,0:T(8,128)(2,1)} %tokens.1, bf16[4096]{0:T(1024)(128)(2,1)} %gain.1, bf16[4096,512]{1,0:T(8,128)(2,1)} %wq.1, bf16[4096,128]{1,0:T(8,128)(2,1)} %wk.1, bf16[4096,128]{1,0:T(8,128)(2,1)} %wv.1, bf16[512,4096]{1,0:T(8,128)(2,1)} %wo.1, s32[8192]{0:T(1024)} %docs.1, ...), custom_call_target="tpu_custom_call" | custom-call | tf_op jit(solution)/shard_map/block/pallas_call | solution.py:461
  50.4 0.8 %copy.11 = bf16[512,512]{1,0:T(8,128)(2,1)} copy(bf16[512,512]{1,0:T(8,128)(2,1)S(1)} %block.1) | data formatting | bytes 1048576

commit v5 on v4

--- a/solution.py
+++ b/solution.py
@@ -26,29 +26,30 @@
 BF16 = jnp.bfloat16
 
 TABLE = [
-    [256, 193, 192, 257, 1271, 16258104, 1270, 1081, 14673980, 16198656, 121, 1198, 1136, 1077, 1199, 1073, 1076, 12968046, 180, 1069, 11969708, 1075, 1330, 15624250],
-    [66, 259, 189, 258, 67, 188, 1345, 1205, 1082, 1088, 1204, 21563, 117, 14131386, 1260, 1074, 1133, 1203, 2102, 12019768, 116, 187, 14575658, 11478127, 1070, 12970032],
-    [260, 69, 186, 68, 261, 187, 1346, 1202, 1081, 1091, 1203, 562232, 13593600, 114, 184, 1281, 1259, 1072, 1024, 1066, 15209649, 115, 11478069, 106, 1324, 2088, 117, 10888237, 2102, 14525492, 12494894],
-    [262, 120, 185, 263, 184, 121, 1025, 1285, 1264, 1024, 257, 1028, 54513, 13052928, 1282, 1192, 1079, 1027, 1065, 562358, 1138, 14491831, 1198, 1323, 1071, 13493299, 1066, 11888684, 2100, 10397734],
-    [328, 137, 567, 136, 329, 566, 1472, 1582, 1073, 1281, 174, 1647, 1072, 71732, 110, 12509359, 1027, 1286, 1709, 14033009, 1026, 1287, 1594599, 258, 1190, 11854892, 112, 1028, 1285, 14193701, 172, 1188, 2088, 10789930, 1323, 13461554],
-    [266, 75, 693, 74, 267, 692, 1475, 1032, 1580, 1074, 1410, 1097, 1581, 611379, 72, 11968684, 1088, 1025, 1412, 71210, 1285, 1125, 1583, 170, 1124, 1195, 9856046, 12413952, 179, 2054, 2082, 1611111, 1062, 10250288, 2088, 10890240],
-    [268, 77, 690, 76, 269, 691, 1220, 1291, 1579, 260, 1157, 1098, 1578, 1153072, 261, 75, 11428011, 1026, 1091, 1414, 611362, 1159, 1577, 258, 98, 2056, 1123, 2151464, 169, 13113344, 168, 106, 9316384, 8727552, 2084, 2094, 12363820, 10332198],
-    [270, 688, 113, 271, 112, 689, 1222, 1293, 1576, 1479, 2056, 1036, 1693225, 262, 168, 3215465, 1028, 1349, 10888353, 2048, 38062, 260, 104, 2058, 1056, 12330159, 2050, 2078, 612013, 1575, 2082, 1702, 2090, 9167916, 11332608, 9807908],
-    [272, 209, 558, 208, 273, 559, 1480, 1063, 1581, 1481, 1062, 551, 2088, 2233388, 614, 10346663, 1088, 1294, 1573, 11870374, 1089, 2058, 1295, 1572, 2625701, 1055, 1350, 164, 2060, 3266592, 8693063, 1054, 2050, 577631, 12097540, 7596060, 2082, 11298858],
-    [338, 556, 173, 339, 172, 557, 1482, 1041, 1060, 1578, 1419, 1040, 81, 1573, 2774059, 80, 548, 9805994, 1091, 1032, 1420, 1571, 1026, 1097, 660749, 131, 1570, 1309, 3216934, 1156, 1052, 9265252, 1029, 2074, 163, 101, 2048, 38926, 7053474, 2054, 1693728, 1063, 2078, 10233896, 10742784],
-    [276, 85, 170, 555, 84, 277, 554, 171, 1484, 1042, 1570, 1064, 1421, 1107, 1059, 3315241, 1181, 82, 9265699, 1098, 1035, 1422, 2774044, 7677327, 75, 1568, 2052, 267, 2064, 1057, 99, 1167528, 161, 98, 2050, 2054, 661512, 2150569, 7088154, 2084, 2086, 10266648, 8071198],
-    [279, 680, 105, 278, 104, 681, 1486, 1045, 6104609, 1487, 2064, 1044, 3855903, 1568, 276, 95, 5378209, 1160, 1036, 1357, 8136222, 1159, 1033, 2200669, 1030, 2066, 4773031, 1190, 2052, 2058, 2659877, 159, 1052, 7660580, 2072, 2082, 6596634, 7105536],
-    [88, 153, 551, 152, 89, 550, 1232, 1056, 6612517, 1233, 1057, 4396580, 9710592, 1054, 96, 545, 1096, 1170, 544, 1097, 1171, 2070, 4788766, 1102, 8053791, 1103, 2058, 3855900, 95, 5330964, 2060, 1677318, 7513117, 2074, 9136162],
-    [91, 548, 165, 90, 164, 549, 154, 539, 1234, 1048, 7120419, 1235, 1049, 4937250, 6450176, 1564, 88, 1226, 1040, 1044, 1163, 1105, 2822682, 1173, 5379616, 1036, 5531166, 140, 1037, 2056, 2199714, 1053, 8627233, 163, 2070, 3856398, 8053791],
-    [93, 546, 163, 92, 162, 547, 156, 541, 1172, 1115, 7627806, 540, 1173, 1114, 5477920, 6990848, 1057, 85, 1100, 538, 158, 1175, 1037, 2066, 3363358, 1561, 1048, 6443169, 4990102, 539, 3856398, 2064, 536, 2058, 2757663, 5975040, 8006656],
-    [158, 96, 545, 543, 160, 97, 94, 544, 161, 1239, 1049, 8135709, 542, 1110, 1048, 6018076, 153, 7541277, 1040, 1563, 150, 6479967, 2062, 1041, 1050, 144, 536, 4313180, 1108, 1045, 540, 5460127, 1036, 1101, 3908121, 2066, 538, 4821085, 6955099, 4893696],
+    [449, 448, 1271, 1081, 16258109, 1270, 1080, 14672956, 121, 1198, 1076, 1072, 16195694, 1073, 113, 180, 1071, 12461109, 1331, 13542450, 2092, 15575098],
+    [322, 323, 189, 188, 1344, 1204, 1083, 116, 187, 1025, 1077, 21562, 117, 14131381, 1075, 1202, 1143, 1078, 13591608, 1081, 2092, 186, 118, 15131952, 2090, 11379761, 12462126],
+    [324, 325, 187, 186, 1346, 1203, 1080, 115, 184, 1027, 1074, 1081, 561411, 13590595, 1280, 1200, 1067, 114, 1076, 1025, 1066, 171, 15208554, 1077, 1073, 11477109, 1132, 13018167, 2088, 1069, 11871286, 12511278],
+    [262, 263, 249, 248, 1284, 1024, 1264, 256, 1025, 1029, 1073, 53377, 261, 13050033, 1026, 1064, 258, 168, 1139, 2102, 10937385, 1283, 561321, 1070, 1074, 174, 2090, 1071, 11429940, 14017575, 2092, 10331174],
+    [456, 457, 567, 566, 1473, 1582, 1072, 174, 110, 1071, 1280, 1585, 71732, 111, 559, 12509359, 1282, 1030, 1127, 14033063, 1581, 1068, 1065, 70, 262, 173, 1027, 1031, 1062, 1593900, 1188, 1284, 10331240, 259, 14193669, 11348010, 1061, 13412402],
+    [331, 330, 692, 693, 1410, 1097, 1580, 1075, 172, 108, 1027, 1069, 1288, 611890, 131, 259, 557, 11968621, 1028, 1025, 1188, 1280, 69697, 1070, 1578, 1195, 110, 265, 1071, 1029, 11428901, 559, 1127, 165, 9822469, 1030, 100, 178, 262, 1031, 1611810, 263, 10774568, 1062, 12904496],
+    [332, 333, 691, 690, 1412, 1099, 1579, 1073, 171, 107, 1029, 1290, 1066, 1072, 1151530, 133, 74, 11428107, 1030, 1186, 1026, 261, 106, 2056, 1580, 1027, 2184233, 1415, 1581, 1064, 1593452, 1059, 2048, 262, 177, 13111395, 1583, 1125, 1070, 11936002, 2080, 1060, 9249027, 8775718, 10267648],
+    [270, 271, 752, 753, 1478, 1032, 1576, 1036, 136, 268, 1031, 1037, 1129, 1033, 1692201, 135, 71, 2199821, 1028, 1035, 1184, 68, 263, 1070, 1579, 2048, 10888222, 1349, 1711, 1053706, 1063, 264, 1066, 11395623, 1069, 557, 267, 2050, 611494, 1068, 11854374, 1055, 2082, 1057, 9168932, 9710592],
+    [558, 464, 465, 559, 1767, 1064, 1288, 1069, 104, 557, 1062, 1161, 1065, 1068, 10346761, 102, 166, 11870758, 1060, 1376, 1025, 164, 552, 1067, 1061, 1039, 2233344, 1249, 2078, 1578, 8691983, 11265356, 1030, 65, 262, 1038, 2082, 7628828, 78, 1287, 3675146, 2050, 2052, 578571, 2659341, 12164096],
+    [339, 338, 685, 684, 1764, 1067, 1291, 1041, 171, 81, 1061, 1578, 1040, 9807114, 101, 170, 549, 4346128, 1058, 1127, 162, 1577, 1288, 2076, 7693352, 1699, 1126, 2050, 9249819, 138, 550, 610384, 1033, 1050, 2080, 2078, 73, 7135371, 72, 8136708, 2060, 1120256, 2054, 104462, 3726336],
+    [341, 340, 683, 682, 1762, 1065, 1298, 1037, 169, 553, 1059, 1107, 1036, 1064, 9265421, 99, 163, 552, 4886796, 1060, 1115, 1156, 1056, 547, 1297, 1050, 1034, 7152655, 1637, 1057, 1182, 1035, 8691983, 1029, 2076, 141, 545, 2723914, 2086, 143, 10199108, 2072, 8070175, 2054, 1040, 1610766, 3807240, 595970],
+    [279, 278, 744, 745, 1760, 1296, 1038, 6104084, 1054, 1041, 1301, 1231, 4379166, 158, 271, 3838046, 1570, 1053, 1030, 1063, 270, 157, 1100, 1049, 268, 153, 78, 1574, 1052, 1037, 7660579, 1183, 1095, 8151583, 1048, 142, 2084, 1569, 9643077, 2074, 7086157, 2056, 1677330, 2058, 4789252, 1137664],
+    [551, 550, 216, 217, 1631, 1040, 6612004, 1057, 1573, 4396241, 545, 97, 1053, 1047, 1032, 541, 87, 1170, 1046, 6071305, 86, 1054, 7595548, 94, 1056, 7088154, 73, 2282517, 1039, 79, 1044, 9087010, 1038, 3838982, 2060, 1031, 1676307, 2775050],
+    [676, 677, 91, 90, 1693, 1107, 7119897, 1052, 1048, 1170, 540, 6529113, 156, 88, 6509083, 1055, 1035, 543, 154, 75, 1034, 2774033, 538, 1187, 2080, 1040, 8544330, 1058, 162, 139, 5531668, 5380118, 1054, 8052883, 2060, 2056, 3330186, 3741710],
+    [546, 547, 221, 220, 1627, 1184, 7627797, 1057, 1626, 7087252, 545, 163, 7049300, 1043, 1042, 162, 83, 4891164, 1049, 2070, 1037, 149, 4886605, 1560, 1036, 6480013, 2078, 6475916, 4450320, 2058, 4297743, 1166, 3759104],
+    [672, 542, 95, 225, 1565, 1239, 8135704, 1052, 1561, 6530262, 540, 94, 7590047, 1040, 1051, 543, 158, 5967963, 1045, 1050, 1041, 536, 85, 7004304, 1044, 1039, 538, 5382228, 1166, 1043, 1042, 78, 4842002, 1037, 1036, 4411469, 3841024, 3300352],
 ]
+CUT = 8
 MARKS = [
-    [4, 6, 6, 6, 6, 6, 6, 6, 6, 6, 8, 6, 6, 8, 8, 9],
-    [5, 11, 20, 19, 29, 31, 29, 28, 34, 40, 37, 30, 31, 35, 34, 37],
-    [9, 15, 24, 23, 34, 34, 33, 31, 36, 200, 41, 35, 200, 200, 200, 200],
-    [22, 200, 200, 200, 200, 200, 200, 200, 200, 200, 200, 200, 200, 200, 200, 200],
-    [24, 26, 31, 30, 36, 36, 38, 36, 38, 45, 43, 38, 35, 37, 37, 40],
+    [2, 4, 4, 4, 4, 4, 4, 4, 4, 4, 4, 4, 4, 4, 4, 4],
+    [4, 11, 22, 22, 34, 40, 35, 38, 37, 39, 42, 40, 31, 33, 28, 32],
+    [8, 14, 25, 25, 36, 42, 39, 41, 40, 41, 45, 42, 33, 36, 31, 36],
+    [18, 25, 200, 200, 200, 200, 200, 200, 200, 200, 200, 200, 200, 200, 200, 200],
+    [22, 27, 32, 32, 38, 45, 45, 46, 46, 45, 48, 46, 38, 38, 33, 38],
 ]
 ENTRIES = max(len(row) for row in TABLE)
 SENDS = [sum((e // (64 << k)) % 2 for e in row for k in range(4)) for row in TABLE]
@@ -83,6 +84,12 @@
     t_dn = lax.rem(z + 3, 4) * 2 + core
     zs = [z, lax.rem(z + 1, 4), lax.rem(z + 3, 4), lax.rem(z + 2, 4)]
     cl, cu = d, 2 * N_CP - 1 - d
+    early = jnp.where(d < CUT, 0, 1)
+    late = 1 - early
+
+    def of(h):
+        return pl.ds(pl.multiple_of(h * STRETCH, STRETCH), STRETCH)
+
     px, py = lax.rem(d, 4), lax.div(d, 4)
     beside = [
         py * 4 + lax.rem(px + 1, 4),
@@ -111,10 +118,11 @@
         cols = pl.ds(pl.multiple_of((2 * i + core) * 512, 512), 512)
         return pltpu.make_async_copy(wo.at[:, cols], wo_own.at[i], wo_sem)
 
-    for c in first_copies:
-        c.start()
+    first_copies[1].start()
     for i in range(N_CHUNK):
         x_copy(i).start()
+    for c in (first_copies[2], first_copies[3], first_copies[0]):
+        c.start()
     for c in rope_copies:
         c.start()
 
@@ -151,15 +159,107 @@
     at_query, at_whole, at_first, at_second, n_entries = [pick(m) for m in MARKS]
     n_sends = pick(SENDS)
 
-    for c in first_copies[:2]:
+    ssq[...] = jnp.zeros_like(ssq)
+    first_copies[1].wait()
+    for i in range(N_CHUNK):
+        cols = slice(i * CHUNK, (i + 1) * CHUNK)
+        gain_row[:, cols] = gain_in[cols].astype(F32).reshape(1, CHUNK)
+
+    def scale_chunk(i):
+        x_copy(i).wait()
+        cols = pl.ds(pl.multiple_of(i * CHUNK, CHUNK), CHUNK)
+        xf = x[:, cols].astype(F32)
+        sq = xf * xf
+        ssq[...] += sq[:, 0:128] + sq[:, 128:256] + sq[:, 256:384] + sq[:, 384:512]
+        xg[:, cols] = (xf * gain_row[:, cols]).astype(BF16)
+
+    def scale_step(i, carry):
+        @pl.when(i == N_CHUNK // 2)
+        def _():
+            wq_copy.start()
+
+        scale_chunk(i)
+        return carry
+
+    lax.fori_loop(0, N_CHUNK, scale_step, 0)
+    for c in first_copies[2:]:
         c.wait()
+    acckv[...] = jnp.dot(xg[...], wkv[...], preferred_element_type=F32)
+    for i in range(4):
+        wo_copy(i).start()
+    for c in rope_copies:
+        c.wait()
+    mean = jnp.sum(ssq[...], axis=1, keepdims=True) * (1.0 / D)
+    factor = lax.rsqrt(mean + EPS)
+    ssq[...] = jnp.broadcast_to(factor, (2 * STRETCH, HD))
+
+    sign = jnp.where(lax.broadcasted_iota(jnp.int32, (1, HD), 1) < HD // 2, -1.0, 1.0)
+
+    def rope(h):
+        c = cl if h == 0 else cu
+        co, so = r_out[0, pl.ds(c, 1), :], r_out[1, pl.ds(c, 1), :]
+        ci, si = r_in[0], r_in[1]
+        return ci * co - si * so, (ci * so + si * co) * sign
+
+    for h, c in ((0, cl), (1, cu)):
+        rs = slice(h * STRETCH, (h + 1) * STRETCH)
+        cosine, sine = rope(h)
+        kf = acckv[rs, 0:HD] * ssq[rs, :]
+        kvbuf[2 * c] = (kf * cosine + pltpu.roll(kf, HD // 2, 1) * sine).astype(BF16)
+        vf = acckv[rs, HD : 2 * HD] * ssq[rs, :]
+        kvbuf[2 * c + 1, 0:HD, :] = vf[0:HD, :].T.astype(BF16)
+        kvbuf[2 * c + 1, HD : 2 * HD, :] = vf[HD : 2 * HD, :].T.astype(BF16)
+
+    pl.semaphore_wait(barrier, 7)
+
+    def kv_slot(p, e):
+        s = lax.div(p, 2)
+        lower = (s < e) & (s >= e - REACH)
+        return lax.rem(s, REACH) * 2 + lax.rem(p, 2) + jnp.where(lower, 0, 2 * REACH)
+
+    def kv_copy(p, way):
+        return pltpu.make_async_remote_copy(
+            src_ref=kvbuf.at[p], dst_ref=kvbuf.at[p], send_sem=kv_send,
+            recv_sem=kv_recv.at[kv_slot(p, beside[way])], device_id={"cp": beside[way], "tp": t},
+        )
+
+    def kv_wait(p):
+        pltpu.make_async_remote_copy(
+            src_ref=kvbuf.at[p], dst_ref=kvbuf.at[p], send_sem=kv_send,
+            recv_sem=kv_recv.at[kv_slot(p, d)], device_id={"cp": beside[0], "tp": t},
+        ).wait_recv()
+
+    def pass_on(e, act):
+        p, ways = lax.rem(e, 64), lax.rem(lax.div(e, 64), 16)
+
+        @pl.when(ways > 0)
+        def _():
+            for way in range(4):
+                @pl.when(lax.rem(lax.div(ways, 2**way), 2) == 1)
+                def _():
+                    act(kv_copy(p, way))
+
+    def send_only(i, carry):
+        pass_on(entry(i), lambda c: c.start())
+        return carry
+
+    lax.fori_loop(0, at_query, send_only, 0)
+
+    def wos_copy(i):
+        cols = pl.ds(pl.multiple_of((2 * i + 1 - core) * 512, 512), 512)
+        return pltpu.make_async_remote_copy(
+            src_ref=wo.at[:, cols], dst_ref=wo_sib.at[i], send_sem=wos_send,
+            recv_sem=wos_recv, device_id={"cp": d, "tp": sib},
+        )
+
+    for i in range(4):
+        wos_copy(i).start()
+
+    first_copies[0].wait()
     table = doc_in[...].reshape(64, 128)
     rows = [
         doc_in[pl.ds(pl.multiple_of(c * STRETCH, STRETCH), STRETCH)].reshape(1, STRETCH) for c in (cl, cu)
     ]
-    for i in range(N_CHUNK):
-        cols = slice(i * CHUNK, (i + 1) * CHUNK)
-        gain_row[:, cols] = gain_in[cols].astype(F32).reshape(1, CHUNK)
     starts = [jnp.zeros((1, STRETCH), F32) for _ in rows]
     for v in range(1, 16):
         below = jnp.where(table < v, 1.0, 0.0)
@@ -169,98 +269,6 @@
     qstart[1:2, :] = starts[1].astype(jnp.int32)
     m_ref[...] = jnp.full_like(m_ref, NEG)
     acc_ref[...] = jnp.zeros_like(acc_ref)
-
-    acckv[...] = jnp.zeros_like(acckv)
-    ssq[...] = jnp.zeros_like(ssq)
-    for c in first_copies[2:]:
-        c.wait()
-
-    def kv_step(i, carry):
-        x_copy(i).wait()
-
-        @pl.when(i == N_CHUNK // 2)
-        def _():
-            wq_copy.start()
-
-        cols = pl.ds(pl.multiple_of(i * CHUNK, CHUNK), CHUNK)
-        xf = x[:, cols].astype(F32)
-        sq = xf * xf
-        ssq[...] += sq[:, 0:128] + sq[:, 128:256] + sq[:, 256:384] + sq[:, 384:512]
-        scaled = (xf * gain_row[:, cols]).astype(BF16)
-        xg[:, cols] = scaled
-        acckv[...] += jnp.dot(scaled, wkv[cols, :], preferred_element_type=F32)
-        return carry
-
-    lax.fori_loop(0, N_CHUNK, kv_step, 0)
-    for i in range(4):
-        wo_copy(i).start()
-    for c in rope_copies:
-        c.wait()
-    mean = jnp.sum(ssq[...], axis=1, keepdims=True) * (1.0 / D)
-    factor = lax.rsqrt(mean + EPS)
-    ssq[...] = jnp.broadcast_to(factor, (2 * STRETCH, HD))
-
-    sign = jnp.where(lax.broadcasted_iota(jnp.int32, (1, HD), 1) < HD // 2, -1.0, 1.0)
-
-    def rope(h):
-        c = cl if h == 0 else cu
-        co, so = r_out[0, pl.ds(c, 1), :], r_out[1, pl.ds(c, 1), :]
-        ci, si = r_in[0], r_in[1]
-        return ci * co - si * so, (ci * so + si * co) * sign
-
-    for h, c in ((0, cl), (1, cu)):
-        rs = slice(h * STRETCH, (h + 1) * STRETCH)
-        cosine, sine = rope(h)
-        kf = acckv[rs, 0:HD] * ssq[rs, :]
-        kvbuf[2 * c] = (kf * cosine + pltpu.roll(kf, HD // 2, 1) * sine).astype(BF16)
-        vf = acckv[rs, HD : 2 * HD] * ssq[rs, :]
-        kvbuf[2 * c + 1, 0:HD, :] = vf[0:HD, :].T.astype(BF16)
-        kvbuf[2 * c + 1, HD : 2 * HD, :] = vf[HD : 2 * HD, :].T.astype(BF16)
-
-    pl.semaphore_wait(barrier, 7)
-
-    def kv_slot(p, e):
-        s = lax.div(p, 2)
-        lower = (s < e) & (s >= e - REACH)
-        return lax.rem(s, REACH) * 2 + lax.rem(p, 2) + jnp.where(lower, 0, 2 * REACH)
-
-    def kv_copy(p, way):
-        return pltpu.make_async_remote_copy(
-            src_ref=kvbuf.at[p], dst_ref=kvbuf.at[p], send_sem=kv_send,
-            recv_sem=kv_recv.at[kv_slot(p, beside[way])], device_id={"cp": beside[way], "tp": t},
-        )
-
-    def kv_wait(p):
-        pltpu.make_async_remote_copy(
-            src_ref=kvbuf.at[p], dst_ref=kvbuf.at[p], send_sem=kv_send,
-            recv_sem=kv_recv.at[kv_slot(p, d)], device_id={"cp": beside[0], "tp": t},
-        ).wait_recv()
-
-    def pass_on(e, act):
-        p, ways = lax.rem(e, 64), lax.rem(lax.div(e, 64), 16)
-
-        @pl.when(ways > 0)
-        def _():
-            for way in range(4):
-                @pl.when(lax.rem(lax.div(ways, 2**way), 2) == 1)
-                def _():
-                    act(kv_copy(p, way))
-
-    def send_only(i, carry):
-        pass_on(entry(i), lambda c: c.start())
-        return carry
-
-    lax.fori_loop(0, at_query, send_only, 0)
-
-    def wos_copy(i):
-        cols = pl.ds(pl.multiple_of((2 * i + 1 - core) * 512, 512), 512)
-        return pltpu.make_async_remote_copy(
-            src_ref=wo.at[:, cols], dst_ref=wo_sib.at[i], send_sem=wos_send,
-            recv_sem=wos_recv, device_id={"cp": d, "tp": sib},
-        )
-
-    for i in range(4):
-        wos_copy(i).start()
 
     wq_copy.wait()
 
@@ -358,22 +366,22 @@
             a_copy(h, way).start()
         for way in range(2):
             near = project(h, 1 + way)
-            accq[h * STRETCH : (h + 1) * STRETCH, way * 256 : (way + 1) * 256] = near[:, summed[way]]
+            accq[of(h), way * 256 : (way + 1) * 256] = near[:, summed[way]]
             send_b[h, way, 1] = near[:, plain[way]].astype(BF16)
             b_copy(h, way, 1).start()
 
     def scatter_second(h):
         for way in range(2):
             a_copy(h, way).wait_recv()
-            own = accq[h * STRETCH : (h + 1) * STRETCH, way * 256 : (way + 1) * 256]
+            own = accq[of(h), way * 256 : (way + 1) * 256]
             send_b[h, way, 0] = (own + recv_a[h, way].astype(F32)).astype(BF16)
             b_copy(h, way, 0).start()
 
     def scatter_mine(h):
-        accq[h * STRETCH : (h + 1) * STRETCH, :] = project(h, 0)
+        accq[of(h), :] = project(h, 0)
 
     def scatter_last(h):
-        rs = slice(h * STRETCH, (h + 1) * STRETCH)
+        rs = of(h)
         pltpu.make_async_copy(recv_b.at[h], recv_b.at[h], b_recv.at[h]).wait()
         out[rs, 0:256] = (
             accq[rs, 0:256] + recv_b[h, 0, 0].astype(F32) + recv_b[h, 1, 1].astype(F32)
@@ -410,41 +418,41 @@
 
         @pl.when(i == at_whole)
         def _():
-            finish(0)
-            at_copy(0).start()
+            finish(early)
+            at_copy(early).start()
 
         @pl.when(i == at_first)
         def _():
             weights_here()
-            scatter_first(0)
+            scatter_first(early)
 
         @pl.when(i == at_second)
         def _():
-            scatter_second(0)
-            scatter_mine(0)
+            scatter_second(early)
+            scatter_mine(early)
 
         return carry
 
     lax.fori_loop(at_query, n_entries, main_step, 0)
-    finish(1)
-    at_copy(1).start()
+    finish(late)
+    at_copy(late).start()
 
     @pl.when(at_first >= n_entries)
     def _():
         weights_here()
-        scatter_first(0)
-
-    scatter_first(1)
+        scatter_first(early)
+
+    scatter_first(late)
 
     @pl.when(at_second >= n_entries)
     def _():
-        scatter_second(0)
-        scatter_mine(0)
-
-    scatter_second(1)
-    scatter_mine(1)
-    scatter_last(0)
-    scatter_last(1)
+        scatter_second(early)
+        scatter_mine(early)
+
+    scatter_second(late)
+    scatter_mine(late)
+    scatter_last(early)
+    scatter_last(late)
     for count in sorted(set(SENDS)):
         @pl.when(n_sends == count)
         def _():

time: 51.3 us -> 48.8 us (0.951); the launches traced: 51.2 us -> 48.2 us
  Pallas kernels: 50.4 us -> 47.4 us
    pallas_call x1, Pallas kernels: 50.4 us -> 47.4 us  [step(): pl.pallas_call(kernel, out_shape=pltpu.VMEM((rows, 512), BF16), in_specs=...]
where the time goes in v5:
time: 48.8 us; the launch traced here: 48.2 us
  Pallas kernels  47.4 us (97%)
  local copies, waits for them, and re-layouts  0.8 us (2%)
    pallas_call x1, Pallas kernels, step(): pl.pallas_call(kernel, out_shape=pltpu.VMEM((rows, 512), BF16), in_specs=...  47.4 us

profile of v5, /device:TPU:24, one launch (start us, length us, event | category | flops | bytes accessed | tf_op | source)
XLA Modules:
  0.0 48.2 jit_solution(11069145683533387712)
XLA Ops:
  0.0 47.4 %block.1 = bf16[512,512]{1,0:T(8,128)(2,1)S(1)} custom-call(bf16[512,4096]{1,0:T(8,128)(2,1)} %tokens.1, bf16[4096]{0:T(1024)(128)(2,1)} %gain.1, bf16[4096,512]{1,0:T(8,128)(2,1)} %wq.1, bf16[4096,128]{1,0:T(8,128)(2,1)} %wk.1, bf16[4096,128]{1,0:T(8,128)(2,1)} %wv.1, bf16[512,4096]{1,0:T(8,128)(2,1)} %wo.1, s32[8192]{0:T(1024)} %docs.1, ...), custom_call_target="tpu_custom_call" | custom-call | tf_op jit(solution)/shard_map/block/pallas_call | solution.py:469
  47.4 0.8 %copy.11 = bf16[512,512]{1,0:T(8,128)(2,1)} copy(bf16[512,512]{1,0:T(8,128)(2,1)S(1)} %block.1) | data formatting | bytes 1048576

commit v6 on v5

--- a/solution.py
+++ b/solution.py
@@ -153,8 +153,8 @@
             i = lax.div(i, 2)
         return values[0]
 
-    def entry(i):
-        return chosen(words, i)
+    def entries(group):
+        return [chosen(words[k::8], group) for k in range(8)]
 
     at_query, at_whole, at_first, at_second, n_entries = [pick(m) for m in MARKS]
     n_sends = pick(SENDS)
@@ -212,21 +212,16 @@
 
     pl.semaphore_wait(barrier, 7)
 
-    def kv_slot(p, e):
-        s = lax.div(p, 2)
-        lower = (s < e) & (s >= e - REACH)
-        return lax.rem(s, REACH) * 2 + lax.rem(p, 2) + jnp.where(lower, 0, 2 * REACH)
-
     def kv_copy(p, way):
         return pltpu.make_async_remote_copy(
             src_ref=kvbuf.at[p], dst_ref=kvbuf.at[p], send_sem=kv_send,
-            recv_sem=kv_recv.at[kv_slot(p, beside[way])], device_id={"cp": beside[way], "tp": t},
+            recv_sem=kv_recv.at[p], device_id={"cp": beside[way], "tp": t},
         )
 
     def kv_wait(p):
         pltpu.make_async_remote_copy(
             src_ref=kvbuf.at[p], dst_ref=kvbuf.at[p], send_sem=kv_send,
-            recv_sem=kv_recv.at[kv_slot(p, d)], device_id={"cp": beside[0], "tp": t},
+            recv_sem=kv_recv.at[p], device_id={"cp": beside[0], "tp": t},
         ).wait_recv()
 
     def pass_on(e, act):
@@ -240,7 +235,7 @@
                     act(kv_copy(p, way))
 
     def send_only(i, carry):
-        pass_on(entry(i), lambda c: c.start())
+        pass_on(chosen(words[:8], i), lambda c: c.start())
         return carry
 
     lax.fori_loop(0, at_query, send_only, 0)
@@ -394,8 +389,8 @@
         pltpu.make_async_copy(wo_own, wo_own, wo_sem).wait()
         pltpu.make_async_copy(wo_sib, wo_sib, wos_recv).wait()
 
-    def main_step(i, carry):
-        e = entry(i)
+    def main_step(i, near):
+        e = chosen(list(near), lax.rem(i, 8))
         p = lax.rem(e, 64)
         kind = lax.rem(lax.div(e, 1024), 4)
         job = lax.rem(lax.div(e, 4096), 4)
@@ -431,9 +426,15 @@
             scatter_second(early)
             scatter_mine(early)
 
+        return near
+
+    def group_step(group, carry):
+        low = jnp.maximum(at_query, group * 8)
+        high = jnp.minimum(n_entries, group * 8 + 8)
+        lax.fori_loop(low, high, main_step, tuple(entries(group)))
         return carry
 
-    lax.fori_loop(at_query, n_entries, main_step, 0)
+    lax.fori_loop(lax.div(at_query, 8), lax.div(n_entries + 7, 8), group_step, 0)
     finish(late)
     at_copy(late).start()
 
@@ -503,7 +504,7 @@
             dma,
             dma,
             dma,
-            dma((4 * REACH,)),
+            dma((4 * N_CP,)),
             dma,
             dma((2,)),
             dma((2, 2)),

time: 48.8 us -> 48.3 us (0.990)
  no operation moved by 1% of the time
where the time goes in v6:
time: 48.3 us; the launch traced here: 48.2 us
  Pallas kernels  47.3 us (98%)
  local copies, waits for them, and re-layouts  0.8 us (2%)
    pallas_call x1, Pallas kernels, step(): pl.pallas_call(kernel, out_shape=pltpu.VMEM((rows, 512), BF16), in_specs=...  47.3 us

profile of v6, /device:TPU:24, one launch (start us, length us, event | category | flops | bytes accessed | tf_op | source)
XLA Modules:
  0.0 48.2 jit_solution(3933018948810925134)
XLA Ops:
  0.0 47.3 %block.1 = bf16[512,512]{1,0:T(8,128)(2,1)S(1)} custom-call(bf16[512,4096]{1,0:T(8,128)(2,1)} %tokens.1, bf16[4096]{0:T(1024)(128)(2,1)} %gain.1, bf16[4096,512]{1,0:T(8,128)(2,1)} %wq.1, bf16[4096,128]{1,0:T(8,128)(2,1)} %wk.1, bf16[4096,128]{1,0:T(8,128)(2,1)} %wv.1, bf16[512,4096]{1,0:T(8,128)(2,1)} %wo.1, s32[8192]{0:T(1024)} %docs.1, ...), custom_call_target="tpu_custom_call" | custom-call | tf_op jit(solution)/shard_map/block/pallas_call | solution.py:470
  47.4 0.8 %copy.11 = bf16[512,512]{1,0:T(8,128)(2,1)} copy(bf16[512,512]{1,0:T(8,128)(2,1)S(1)} %block.1) | data formatting | bytes 1048576

commit v7 on v6

--- a/solution.py
+++ b/solution.py
@@ -26,30 +26,30 @@
 BF16 = jnp.bfloat16
 
 TABLE = [
-    [449, 448, 1271, 1081, 16258109, 1270, 1080, 14672956, 121, 1198, 1076, 1072, 16195694, 1073, 113, 180, 1071, 12461109, 1331, 13542450, 2092, 15575098],
-    [322, 323, 189, 188, 1344, 1204, 1083, 116, 187, 1025, 1077, 21562, 117, 14131381, 1075, 1202, 1143, 1078, 13591608, 1081, 2092, 186, 118, 15131952, 2090, 11379761, 12462126],
-    [324, 325, 187, 186, 1346, 1203, 1080, 115, 184, 1027, 1074, 1081, 561411, 13590595, 1280, 1200, 1067, 114, 1076, 1025, 1066, 171, 15208554, 1077, 1073, 11477109, 1132, 13018167, 2088, 1069, 11871286, 12511278],
-    [262, 263, 249, 248, 1284, 1024, 1264, 256, 1025, 1029, 1073, 53377, 261, 13050033, 1026, 1064, 258, 168, 1139, 2102, 10937385, 1283, 561321, 1070, 1074, 174, 2090, 1071, 11429940, 14017575, 2092, 10331174],
-    [456, 457, 567, 566, 1473, 1582, 1072, 174, 110, 1071, 1280, 1585, 71732, 111, 559, 12509359, 1282, 1030, 1127, 14033063, 1581, 1068, 1065, 70, 262, 173, 1027, 1031, 1062, 1593900, 1188, 1284, 10331240, 259, 14193669, 11348010, 1061, 13412402],
-    [331, 330, 692, 693, 1410, 1097, 1580, 1075, 172, 108, 1027, 1069, 1288, 611890, 131, 259, 557, 11968621, 1028, 1025, 1188, 1280, 69697, 1070, 1578, 1195, 110, 265, 1071, 1029, 11428901, 559, 1127, 165, 9822469, 1030, 100, 178, 262, 1031, 1611810, 263, 10774568, 1062, 12904496],
-    [332, 333, 691, 690, 1412, 1099, 1579, 1073, 171, 107, 1029, 1290, 1066, 1072, 1151530, 133, 74, 11428107, 1030, 1186, 1026, 261, 106, 2056, 1580, 1027, 2184233, 1415, 1581, 1064, 1593452, 1059, 2048, 262, 177, 13111395, 1583, 1125, 1070, 11936002, 2080, 1060, 9249027, 8775718, 10267648],
-    [270, 271, 752, 753, 1478, 1032, 1576, 1036, 136, 268, 1031, 1037, 1129, 1033, 1692201, 135, 71, 2199821, 1028, 1035, 1184, 68, 263, 1070, 1579, 2048, 10888222, 1349, 1711, 1053706, 1063, 264, 1066, 11395623, 1069, 557, 267, 2050, 611494, 1068, 11854374, 1055, 2082, 1057, 9168932, 9710592],
-    [558, 464, 465, 559, 1767, 1064, 1288, 1069, 104, 557, 1062, 1161, 1065, 1068, 10346761, 102, 166, 11870758, 1060, 1376, 1025, 164, 552, 1067, 1061, 1039, 2233344, 1249, 2078, 1578, 8691983, 11265356, 1030, 65, 262, 1038, 2082, 7628828, 78, 1287, 3675146, 2050, 2052, 578571, 2659341, 12164096],
-    [339, 338, 685, 684, 1764, 1067, 1291, 1041, 171, 81, 1061, 1578, 1040, 9807114, 101, 170, 549, 4346128, 1058, 1127, 162, 1577, 1288, 2076, 7693352, 1699, 1126, 2050, 9249819, 138, 550, 610384, 1033, 1050, 2080, 2078, 73, 7135371, 72, 8136708, 2060, 1120256, 2054, 104462, 3726336],
-    [341, 340, 683, 682, 1762, 1065, 1298, 1037, 169, 553, 1059, 1107, 1036, 1064, 9265421, 99, 163, 552, 4886796, 1060, 1115, 1156, 1056, 547, 1297, 1050, 1034, 7152655, 1637, 1057, 1182, 1035, 8691983, 1029, 2076, 141, 545, 2723914, 2086, 143, 10199108, 2072, 8070175, 2054, 1040, 1610766, 3807240, 595970],
-    [279, 278, 744, 745, 1760, 1296, 1038, 6104084, 1054, 1041, 1301, 1231, 4379166, 158, 271, 3838046, 1570, 1053, 1030, 1063, 270, 157, 1100, 1049, 268, 153, 78, 1574, 1052, 1037, 7660579, 1183, 1095, 8151583, 1048, 142, 2084, 1569, 9643077, 2074, 7086157, 2056, 1677330, 2058, 4789252, 1137664],
-    [551, 550, 216, 217, 1631, 1040, 6612004, 1057, 1573, 4396241, 545, 97, 1053, 1047, 1032, 541, 87, 1170, 1046, 6071305, 86, 1054, 7595548, 94, 1056, 7088154, 73, 2282517, 1039, 79, 1044, 9087010, 1038, 3838982, 2060, 1031, 1676307, 2775050],
-    [676, 677, 91, 90, 1693, 1107, 7119897, 1052, 1048, 1170, 540, 6529113, 156, 88, 6509083, 1055, 1035, 543, 154, 75, 1034, 2774033, 538, 1187, 2080, 1040, 8544330, 1058, 162, 139, 5531668, 5380118, 1054, 8052883, 2060, 2056, 3330186, 3741710],
-    [546, 547, 221, 220, 1627, 1184, 7627797, 1057, 1626, 7087252, 545, 163, 7049300, 1043, 1042, 162, 83, 4891164, 1049, 2070, 1037, 149, 4886605, 1560, 1036, 6480013, 2078, 6475916, 4450320, 2058, 4297743, 1166, 3759104],
-    [672, 542, 95, 225, 1565, 1239, 8135704, 1052, 1561, 6530262, 540, 94, 7590047, 1040, 1051, 543, 158, 5967963, 1045, 1050, 1041, 536, 85, 7004304, 1044, 1039, 538, 5382228, 1166, 1043, 1042, 78, 4842002, 1037, 1036, 4411469, 3841024, 3300352],
+    [448, 449, 16260096, 1270, 1079, 2104, 14673980, 1262, 1073, 16196660, 183, 1136, 12461103, 111, 1077, 175, 181, 119, 1196, 11969581, 2098, 15624250],
+    [323, 322, 188, 189, 1345, 1204, 1082, 116, 186, 1077, 1083, 21504, 117, 14131381, 1068, 1075, 1261, 12018745, 1074, 178, 108, 1070, 1080, 15098043, 2096, 1135, 12462122, 14510134],
+    [324, 325, 186, 187, 1347, 1203, 1081, 115, 185, 1026, 1074, 562232, 66, 13590706, 1281, 1024, 1066, 106, 15208632, 1073, 1067, 1140, 11477169, 1077, 1072, 13017202, 1069, 2088, 109, 11871276, 2102, 12511278],
+    [262, 263, 249, 248, 1284, 1152, 1137, 177, 1029, 1281, 1072, 1101936, 261, 13050032, 1027, 1064, 259, 168, 1078, 1139, 182, 1065, 529410, 1198, 1207, 1071, 2090, 14492724, 11398144, 1077, 13542450, 2092, 10332198],
+    [456, 457, 566, 567, 1472, 1582, 1072, 110, 174, 1025, 1071, 1073, 2100, 559, 69889, 111, 12509359, 1286, 1026, 70, 14033026, 1580, 1064, 1065, 172, 105, 1283, 1031, 2086, 1593415, 263, 1028, 1197, 10297457, 260, 1061, 165, 9806884, 14193925, 2090, 13461554],
+    [331, 330, 692, 693, 1474, 1032, 1580, 1074, 72, 172, 1027, 1069, 1289, 1075, 610861, 131, 109, 11968771, 1028, 1024, 1061, 1025, 132, 64, 69896, 1578, 1070, 1067, 165, 108, 11428100, 1029, 1060, 1071, 111, 261, 178, 12362283, 1062, 1030, 102, 257, 179, 2082, 1611015, 1063, 2088, 10250288, 12921856],
+    [333, 332, 691, 690, 1412, 1099, 1578, 1072, 170, 267, 1029, 1034, 1131, 1073, 1151531, 133, 74, 11428101, 1030, 1026, 1058, 1027, 262, 176, 610410, 1577, 2056, 259, 162, 98, 1031, 1643560, 2048, 263, 168, 13112419, 2080, 2092, 10887426, 2094, 2084, 8676390, 12430336, 10265639],
+    [271, 270, 753, 752, 1478, 1033, 1037, 1576, 137, 269, 1031, 1036, 1129, 1032, 1692201, 135, 71, 2199815, 1028, 1035, 1185, 10887435, 1070, 1643, 2048, 260, 1184, 1029, 1071, 1034, 69, 174, 265, 1053727, 2050, 1066, 610565, 1574, 12330018, 1191, 2092, 1059, 10314279, 2084, 9282590, 8170496],
+    [558, 559, 465, 464, 1766, 1064, 1289, 1068, 104, 552, 1063, 1069, 1160, 1065, 10346760, 103, 167, 10854951, 1061, 1060, 1121, 1024, 164, 2232877, 1025, 1359, 1067, 1056, 165, 8692260, 1055, 1066, 1054, 95, 8217130, 1286, 2082, 64, 1034, 266, 70, 3675150, 2050, 7628828, 1287, 1035, 1594381, 1036, 3233796, 12098560],
+    [339, 684, 338, 685, 1765, 1067, 1291, 1040, 171, 555, 1060, 1066, 1098, 9807121, 100, 170, 266, 2773540, 1062, 1058, 1154, 102, 550, 9266211, 1289, 2088, 138, 80, 547, 1052, 1063, 1037, 1027, 269, 156, 103, 10297895, 1036, 1032, 2080, 268, 141, 659528, 1039, 1053, 73, 7610639, 2074, 2078, 8087556, 1038, 2201600, 3708934, 1580032],
+    [683, 682, 341, 340, 1762, 1065, 1298, 1037, 169, 553, 1059, 1100, 1043, 1064, 9265421, 99, 268, 141, 3314216, 1061, 1052, 92, 140, 1053, 7676451, 1290, 1035, 2080, 157, 549, 2773074, 1050, 1060, 2052, 90, 9708068, 1166, 2078, 74, 1051, 7070736, 1039, 3708966, 2054, 6613016, 2050, 1041, 579592, 2235392],
+    [744, 745, 278, 279, 6106112, 1761, 1295, 1044, 1056, 1038, 1045, 2064, 270, 160, 79, 3854880, 277, 1055, 95, 159, 4362783, 1058, 1062, 1054, 276, 98, 142, 8135206, 1037, 1036, 78, 269, 143, 1049, 1575, 2054, 9233443, 1099, 1572, 2076, 1675417, 1048, 1061, 76, 6529566, 2056, 7120922, 1120260, 1034, 4806674],
+    [550, 551, 216, 217, 6614016, 1572, 1120, 1169, 1040, 1054, 1061, 544, 94, 4395152, 542, 80, 1055, 8168474, 1033, 95, 1571, 1053, 1032, 72, 541, 1057, 7611420, 1110, 1058, 6054935, 5837851, 5466132, 2062, 3838987, 1034, 2066, 4805645, 2054, 3200012],
+    [677, 676, 90, 91, 539, 7119002, 1059, 1107, 1049, 547, 163, 1052, 1048, 4924434, 540, 88, 6508700, 1058, 1035, 162, 1568, 89, 7627805, 1566, 155, 75, 1044, 1034, 2064, 538, 2773140, 1057, 1055, 8134795, 1045, 2056, 5378194, 1037, 5941270, 5837964, 3774478],
+    [546, 675, 220, 93, 162, 7627292, 1054, 1114, 1045, 541, 157, 1051, 1057, 5465108, 91, 538, 7049364, 1056, 1042, 542, 161, 82, 4989971, 1037, 1055, 83, 539, 4886677, 1048, 1047, 1036, 536, 151, 76, 6022166, 5870617, 1553, 2824202, 4400144, 1166, 3806223],
+    [673, 608, 222, 543, 95, 8134816, 1053, 1046, 1048, 542, 159, 93, 1052, 1049, 6530071, 97, 151, 7590425, 150, 541, 5967958, 1041, 1050, 1039, 536, 87, 145, 1038, 3859472, 1051, 144, 1109, 6955547, 1042, 78, 4313230, 1044, 1555, 143, 4890707, 1037, 77, 5461004, 3300352],
 ]
 CUT = 8
 MARKS = [
-    [2, 4, 4, 4, 4, 4, 4, 4, 4, 4, 4, 4, 4, 4, 4, 4],
-    [4, 11, 22, 22, 34, 40, 35, 38, 37, 39, 42, 40, 31, 33, 28, 32],
-    [8, 14, 25, 25, 36, 42, 39, 41, 40, 41, 45, 42, 33, 36, 31, 36],
-    [18, 25, 200, 200, 200, 200, 200, 200, 200, 200, 200, 200, 200, 200, 200, 200],
-    [22, 27, 32, 32, 38, 45, 45, 46, 46, 45, 48, 46, 38, 38, 33, 38],
+    [2, 4, 4, 4, 4, 4, 4, 4, 4, 4, 4, 4, 4, 4, 4, 3],
+    [2, 11, 18, 22, 38, 44, 35, 36, 43, 49, 44, 46, 31, 38, 38, 39],
+    [6, 15, 22, 23, 200, 200, 38, 39, 46, 51, 47, 200, 33, 39, 200, 200],
+    [17, 24, 29, 31, 200, 200, 200, 200, 200, 200, 200, 200, 200, 200, 200, 200],
+    [22, 28, 32, 33, 41, 49, 44, 46, 50, 54, 49, 50, 39, 41, 41, 44],
 ]
 ENTRIES = max(len(row) for row in TABLE)
 SENDS = [sum((e // (64 << k)) % 2 for e in row for k in range(4)) for row in TABLE]
@@ -72,7 +72,7 @@
     tokens, gain, wq, wk, wv, wo, docs, rope_in, rope_out, out,
     x, xg, wkv, wqv, wo_own, wo_sib, acckv, accq, ssq, kvbuf, qs,
     m_ref, acc_ref, attn_own, attn_sib, send_a, recv_a, send_b, recv_b, qstart,
-    gain_in, gain_row, doc_in, r_in, r_out,
+    gain_in, gain_row, doc_in, r_in, r_out, part,
     in_sems, x_sems, wo_sem, wos_send, wos_recv, kv_send, kv_recv,
     rs_send, at_recv, a_recv, b_recv,
 ):
@@ -353,14 +353,21 @@
     summed = [slice(0, 256), slice(256, 512)]
     plain = [slice(256, 512), slice(0, 256)]
 
+    def own_part(h):
+        for j, i in enumerate((3, 1, 2)):
+            part[j] = jnp.dot(attn_own[h], wo_own[zs[i]], preferred_element_type=F32)
+
+    def with_sibling(h, j, i):
+        return part[j] + jnp.dot(attn_sib[h], wo_sib[zs[i]], preferred_element_type=F32)
+
     def scatter_first(h):
         at_copy(h).wait_recv()
-        far = project(h, 3)
+        far = with_sibling(h, 0, 3)
         for way in range(2):
             send_a[h, way] = far[:, summed[way]].astype(BF16)
             a_copy(h, way).start()
         for way in range(2):
-            near = project(h, 1 + way)
+            near = with_sibling(h, 1 + way, 1 + way)
             accq[of(h), way * 256 : (way + 1) * 256] = near[:, summed[way]]
             send_b[h, way, 1] = near[:, plain[way]].astype(BF16)
             b_copy(h, way, 1).start()
@@ -386,7 +393,6 @@
         ).astype(BF16)
 
     def weights_here():
-        pltpu.make_async_copy(wo_own, wo_own, wo_sem).wait()
         pltpu.make_async_copy(wo_sib, wo_sib, wos_recv).wait()
 
     def main_step(i, near):
@@ -415,6 +421,8 @@
         def _():
             finish(early)
             at_copy(early).start()
+            pltpu.make_async_copy(wo_own, wo_own, wo_sem).wait()
+            own_part(early)
 
         @pl.when(i == at_first)
         def _():
@@ -443,6 +451,7 @@
         weights_here()
         scatter_first(early)
 
+    own_part(late)
     scatter_first(late)
 
     @pl.when(at_second >= n_entries)
@@ -498,6 +507,7 @@
             pltpu.VMEM((2 * N_CP * STRETCH,), jnp.int32),
             pltpu.VMEM((2, STRETCH, HD), F32),
             pltpu.VMEM((2, 2 * N_CP, HD), F32),
+            pltpu.VMEM((3, STRETCH, 512), F32),
             dma((7,)),
             dma((N_CHUNK,)),
             dma,

time: 48.3 us -> 48 us (level)
  no operation moved by 1% of the time
where the time goes in v7:
time: 48 us; the launch traced here: 47.8 us
  Pallas kernels  47 us (98%)
  local copies, waits for them, and re-layouts  0.8 us (2%)
    pallas_call x1, Pallas kernels, step(): pl.pallas_call(kernel, out_shape=pltpu.VMEM((rows, 512), BF16), in_specs=...  47 us

profile of v7, /device:TPU:24, one launch (start us, length us, event | category | flops | bytes accessed | tf_op | source)
XLA Modules:
  0.0 47.8 jit_solution(12610372503718662799)
XLA Ops:
  0.0 47.0 %block.1 = bf16[512,512]{1,0:T(8,128)(2,1)S(1)} custom-call(bf16[512,4096]{1,0:T(8,128)(2,1)} %tokens.1, bf16[4096]{0:T(1024)(128)(2,1)} %gain.1, bf16[4096,512]{1,0:T(8,128)(2,1)} %wq.1, bf16[4096,128]{1,0:T(8,128)(2,1)} %wk.1, bf16[4096,128]{1,0:T(8,128)(2,1)} %wv.1, bf16[512,4096]{1,0:T(8,128)(2,1)} %wo.1, s32[8192]{0:T(1024)} %docs.1, ...), custom_call_target="tpu_custom_call" | custom-call | tf_op jit(solution)/shard_map/block/pallas_call | solution.py:479
  47.0 0.8 %copy.11 = bf16[512,512]{1,0:T(8,128)(2,1)} copy(bf16[512,512]{1,0:T(8,128)(2,1)S(1)} %block.1) | data formatting | bytes 1048576

commit v8 on v7

--- a/solution.py
+++ b/solution.py
@@ -174,7 +174,7 @@
         xg[:, cols] = (xf * gain_row[:, cols]).astype(BF16)
 
     def scale_step(i, carry):
-        @pl.when(i == N_CHUNK // 2)
+        @pl.when(i == N_CHUNK - 1)
         def _():
             wq_copy.start()
 

time: 48 us -> 48 us (level)
  no operation moved by 1% of the time
where the time goes in v8:
time: 48 us; the launch traced here: 47.8 us
  Pallas kernels  47 us (98%)
  local copies, waits for them, and re-layouts  0.8 us (2%)
    pallas_call x1, Pallas kernels, step(): pl.pallas_call(kernel, out_shape=pltpu.VMEM((rows, 512), BF16), in_specs=...  47 us

profile of v8, /device:TPU:24, one launch (start us, length us, event | category | flops | bytes accessed | tf_op | source)
XLA Modules:
  0.0 47.8 jit_solution(14281870305136367984)
XLA Ops:
  0.0 47.0 %block.1 = bf16[512,512]{1,0:T(8,128)(2,1)S(1)} custom-call(bf16[512,4096]{1,0:T(8,128)(2,1)} %tokens.1, bf16[4096]{0:T(1024)(128)(2,1)} %gain.1, bf16[4096,512]{1,0:T(8,128)(2,1)} %wq.1, bf16[4096,128]{1,0:T(8,128)(2,1)} %wk.1, bf16[4096,128]{1,0:T(8,128)(2,1)} %wv.1, bf16[512,4096]{1,0:T(8,128)(2,1)} %wo.1, s32[8192]{0:T(1024)} %docs.1, ...), custom_call_target="tpu_custom_call" | custom-call | tf_op jit(solution)/shard_map/block/pallas_call | solution.py:479
  47.0 0.8 %copy.11 = bf16[512,512]{1,0:T(8,128)(2,1)} copy(bf16[512,512]{1,0:T(8,128)(2,1)S(1)} %block.1) | data formatting | bytes 1048576
